TPU v7x, 32 devices: a whole 2x2x4 slice. The times are simulated.
32 devices in a mesh: cells: 8 (over z, y), coef: 4 (over x, core).
Axes of the slice: x: 2, y: 2, z: 4, core: 2. Of those that a mesh axis runs over, the one named last changes fastest.
Arguments:
- multipole: bfloat16 [128, 1024], P('coef', 'cells'), may hold values from -6 to 6
- parent_local: bfloat16 [128, 128], P('coef', 'cells'), may hold values from -6 to 6
- m2l_ops: bfloat16 [189, 128, 128], P(None, 'coef'), may hold values from -0.0390625 to 0.0390625
- l2l_ops: bfloat16 [8, 128, 128], P(None, 'coef'), may hold values from -0.5 to 0.5
- target_cell: int32 [189, 1024], P(None, 'cells'), may hold values from -1 to 1023, as said below
- particle_leaf: int32 [16384], P('cells'), may hold values from 0 to 1023, as said below
- particle_basis: bfloat16 [128, 16384], P('coef', 'cells'), may hold values from -0.5 to 0.5
Outputs:
- leaf_local: float32 [128, 1024], P('coef', 'cells')
- potential: float32 [16384], P('cells')
Inputs may be any that keep to these rules, and one draw needn't show every extreme that they name: `target_cell`: -1 marks an empty slot. Otherwise the target of source cell c lies on the device of c (cells are owned in blocks of 128: device c // 128) or on a device at most 2 indices away; from one device's source cells at most 256 pairs target the cells of any one other device, and some pair of devices has exactly 256. `particle_leaf`: the particles at positions d * 2048 to (d + 1) * 2048 - 1 lie in cells d * 128 to (d + 1) * 128 - 1.
All inputs are finite; a program needn't handle non-finite values.
Results may differ from a plain program's by a relative error of at most 0.0003.
Values may be sent and summed in bfloat16 or wider, within the bound.
No kernel may reach another device: no remote copies, remote signals or barrier semaphores. Data moves between devices by JAX's collectives and lax.ppermute only.
A program may use at most 64 MiB of HBM per device.

v0:
```python
import jax
import jax.numpy as jnp
from jax import lax
from jax.sharding import PartitionSpec as P

REACH = 2


def passed_along(value, axis, steps):
    count = lax.axis_size(axis)
    first, last = (max(0, -steps), min(count, count - steps))
    return lax.ppermute(value, axis, [(source, source + steps) for source in range(first, last)])


def on_device(
    multipole, parent_local, m2l_ops, l2l_ops, target_cell, particle_leaf, particle_basis
):
    my_index = lax.axis_index("cells")
    cells_dev = multipole.shape[1]
    full_poles, full_parents = (
        lax.all_gather(multipole, "coef", axis=0, tiled=True),
        lax.all_gather(parent_local, "coef", axis=0, tiled=True),
    )
    translated = jnp.einsum("oqk,kc->qoc", m2l_ops, full_poles, preferred_element_type=jnp.float32)
    coef_share = translated.shape[0]
    flat_terms = translated.reshape(coef_share, -1)
    targets = target_cell.reshape(-1)
    first_cell = my_index * cells_dev
    distances = []
    for length in range(1, REACH + 1):
        for direction in (1, -1):
            distances.append(length * direction)
    span = (2 * REACH + 1) * cells_dev
    lowest = (my_index - REACH) * cells_dev
    wide_index = jnp.where(targets >= 0, targets - lowest, span)
    wide_sums = (
        jnp.zeros((coef_share, span), jnp.float32).at[:, wide_index].add(flat_terms, mode="drop")
    )
    m2l_sum = wide_sums[:, REACH * cells_dev : (REACH + 1) * cells_dev]
    for distance in distances:
        offset = (REACH + distance) * cells_dev
        outgoing = wide_sums[:, offset : offset + cells_dev]
        m2l_sum = m2l_sum + passed_along(outgoing, "cells", distance)
    shifted = jnp.einsum("oqk,kp->qpo", l2l_ops, full_parents, preferred_element_type=jnp.float32)
    leaf_local = m2l_sum + shifted.reshape(coef_share, cells_dev)
    leaf_index = particle_leaf - first_cell
    columns = leaf_local[:, leaf_index]
    partial_sum = jnp.sum(columns * particle_basis.astype(jnp.float32), axis=0)
    potential = lax.psum(partial_sum, "coef")
    return (leaf_local, potential)


def solution(mesh):
    return jax.shard_map(
        on_device,
        mesh=mesh,
        in_specs=(
            P("coef", "cells"),
            P("coef", "cells"),
            P(None, "coef", None),
            P(None, "coef", None),
            P(None, "cells"),
            P("cells"),
            P("coef", "cells"),
        ),
        out_specs=(P("coef", "cells"), P("cells")),
        check_vma=False,
    )
```

profile of v0, /device:TPU:0, one launch (start us, length us, event | category | flops | bytes accessed | tf_op | source)
XLA Modules:
  0.0 183.9 jit_solution(15182055329372651720)
XLA Ops:
  0.6 0.0 copy-start
  0.7 1.0 select_bitcast_fusion
  1.7 0.3 fusion.5
  2.0 6.4 %all_gather.6 = bf16[128,128]{1,0:T(8,128)(2,1)S(1)} all-gather(bf16[32,128]{1,0:T(8,128)(2,1)} %param.7), channel_id=1, replica_groups=mesh['cells'=8,'coef'=4] {'coef'}, dimensions={0}, use_global_device_ids=true | all-gather | bytes 40960 | tf_op jit(solution)/shard_map/all_gather | solution.py:21
  8.4 0.0 copy-done
  8.4 0.7 fusion
  9.1 3.5 %copy.39 = f32[4,8,189,128]{3,1,2,0:T(8,128)} copy(f32[4,8,189,128]{3,2,1,0:T(8,128)S(1)} %bitcast.30) | data formatting | bytes 6193152
  12.6 0.0 copy-start.4
  12.6 0.0 copy-start.2
  12.6 0.0 copy-start.3
  12.6 7.7 %copy.27 = f32[24192,32]{1,0:T(8,128)} copy(f32[24192,32]{0,1:T(8,128)} %bitcast.31) | data formatting | bytes 6193152 | tf_op jit(solution)/shard_map/reshape | solution.py:26
  20.3 0.0 copy-start.1
  20.3 131.6 %scatter_custom_fusion = f32[32,640]{0,1:T(8,128)S(1)} fusion(s32[24192]{0:T(1024)S(1)} %fusion.5, f32[24192,32]{1,0:T(8,128)} %copy.27, f32[]{:T(128)} %constant.7.clone.1), kind=kCustom, calls=%fused_computation.9 | custom fusion | flops 774144 | bytes 82432 | tf_op jit(solution)/shard_map/scatter-add | solution.py:37
  151.9 3.9 %collective-permute-start = (f32[32,128]{0,1:T(8,128)S(1)}, f32[32,128]{0,1:T(8,128)S(1)}, u32[]{:S(2)}, u32[]{:S(2)}) collective-permute-start(f32[32,128]{0,1:T(8,128)S(1)} %get-tuple-element.10), channel_id=1, source_target_pairs={{0,4},{4,8},{8,12},{12,16},{16,20},{20,24},{24,28},{1,5},{5,9},{9,... | collective-permute-start | bytes 49160 | tf_op jit(solution)/shard_map/ppermute | solution.py:12
  155.8 1.3 collective-permute-start.1
  157.1 5.5 %collective-permute-start.2 = (f32[32,128]{0,1:T(8,128)S(1)}, f32[32,128]{0,1:T(8,128)S(1)}, u32[]{:S(2)}, u32[]{:S(2)}) collective-permute-start(f32[32,128]{0,1:T(8,128)S(1)} %get-tuple-element.12), channel_id=1, source_target_pairs={{0,8},{4,12},{8,16},{12,20},{16,24},{20,28},{1,9},{5,13},{9,17},{1... | collective-permute-start | bytes 49160 | tf_op jit(solution)/shard_map/ppermute | solution.py:12
  162.6 1.3 collective-permute-start.3
  163.9 0.0 copy-done.4
  164.0 5.2 %all-gather = bf16[4,32,16]{1,2,0:T(8,128)(2,1)S(1)} all-gather(bf16[1,32,16]{1,2,0:T(8,128)(2,1)S(1)} %bitcast.32), channel_id=1, replica_groups=mesh['cells'=8,'coef'=4] {'coef'}, dimensions={0}, use_global_device_ids=true | all-gather | bytes 5120 | tf_op jit(solution)/shard_map/all_gather | solution.py:22
  169.2 0.1 reshape.70
  169.3 0.0 copy-done.2
  169.3 0.2 convolution_bitcast_fusion
  169.4 0.0 copy-done.3
  169.5 0.0 collective-permute-done
  169.5 0.0 collective-permute-done.1
  169.5 0.0 collective-permute-done.2
  169.5 0.0 collective-permute-done.3
  169.6 0.7 copy.31
  170.2 5.5 %gather_fusion = f32[2048,32]{1,0:T(8,128)S(1)} fusion(f32[32,128]{0,1:T(8,128)S(1)} %fusion.9, s32[2048]{0:T(1024)S(1)} %fusion.11), kind=kCustom, calls=%fused_computation | custom fusion | bytes 532480 | tf_op jit(solution)/shard_map/gather | solution.py:47
  175.7 0.3 copy.30
  176.0 0.0 copy-done.1
  176.0 0.1 fusion.2
  176.1 7.8 %psum.7 = f32[2048]{0:T(1024)} all-reduce(f32[2048]{0:T(1024)S(1)} %fusion.2), channel_id=1, replica_groups=mesh['cells'=8,'coef'=4] {'coef'}, use_global_device_ids=true, to_apply=%region_2.3 | all-reduce | flops 2048 | bytes 16384 | tf_op jit(solution)/shard_map/psum | solution.py:49
  (4 shorter events, 0.1 us)
Async XLA Ops:
  0.6 7.8 %copy-start = (bf16[189,32,128]{2,1,0:T(8,128)(2,1)S(1)}, bf16[189,32,128]{2,1,0:T(8,128)(2,1)}, u32[]{:S(2)}) copy-start(bf16[189,32,128]{2,1,0:T(8,128)(2,1)} %param.9) | copy-start | bytes 4644868
  12.6 151.4 %copy-start.4 = (bf16[32,16]{0,1:T(8,128)(2,1)S(1)}, bf16[32,16]{0,1:T(8,128)(2,1)}, u32[]{:S(2)}) copy-start(bf16[32,16]{0,1:T(8,128)(2,1)} %param.8) | copy-start | bytes 3076
  12.6 156.7 %copy-start.2 = (bf16[8,32,128]{2,1,0:T(8,128)(2,1)S(1)}, bf16[8,32,128]{2,1,0:T(8,128)(2,1)}, u32[]{:S(2)}) copy-start(bf16[8,32,128]{2,1,0:T(8,128)(2,1)} %param.10) | copy-start | bytes 196612
  12.6 156.9 %copy-start.3 = (s32[2048]{0:T(1024)S(1)}, s32[2048]{0:T(1024)}, u32[]{:S(2)}) copy-start(s32[2048]{0:T(1024)} %param.12) | copy-start | bytes 24580
  20.3 155.7 %copy-start.1 = (bf16[32,2048]{1,0:T(8,128)(2,1)S(1)}, bf16[32,2048]{1,0:T(8,128)(2,1)}, u32[]{:S(2)}) copy-start(bf16[32,2048]{1,0:T(8,128)(2,1)} %param.13) | copy-start | bytes 393220
  151.9 17.5 %collective-permute-start = (f32[32,128]{0,1:T(8,128)S(1)}, f32[32,128]{0,1:T(8,128)S(1)}, u32[]{:S(2)}, u32[]{:S(2)}) collective-permute-start(f32[32,128]{0,1:T(8,128)S(1)} %get-tuple-element.10), channel_id=1, source_target_pairs={{0,4},{4,8},{8,12},{12,16},{16,20},{20,24},{24,28},{1,5},{5,9},{9,... | collective-permute-start | bytes 49160 | tf_op jit(solution)/shard_map/ppermute | solution.py:12
  155.8 13.7 %collective-permute-start.1 = (f32[32,128]{0,1:T(8,128)S(1)}, f32[32,128]{0,1:T(8,128)S(1)}, u32[]{:S(2)}, u32[]{:S(2)}) collective-permute-start(f32[32,128]{0,1:T(8,128)S(1)} %get-tuple-element.13), channel_id=1, source_target_pairs={{4,0},{8,4},{12,8},{16,12},{20,16},{24,20},{28,24},{5,1},{9,5},{13... | collective-permute-start | bytes 49160 | tf_op jit(solution)/shard_map/ppermute | solution.py:12
  157.1 12.4 %collective-permute-start.2 = (f32[32,128]{0,1:T(8,128)S(1)}, f32[32,128]{0,1:T(8,128)S(1)}, u32[]{:S(2)}, u32[]{:S(2)}) collective-permute-start(f32[32,128]{0,1:T(8,128)S(1)} %get-tuple-element.12), channel_id=1, source_target_pairs={{0,8},{4,12},{8,16},{12,20},{16,24},{20,28},{1,9},{5,13},{9,17},{1... | collective-permute-start | bytes 49160 | tf_op jit(solution)/shard_map/ppermute | solution.py:12
  162.6 6.9 %collective-permute-start.3 = (f32[32,128]{0,1:T(8,128)S(1)}, f32[32,128]{0,1:T(8,128)S(1)}, u32[]{:S(2)}, u32[]{:S(2)}) collective-permute-start(f32[32,128]{0,1:T(8,128)S(1)} %get-tuple-element.11), channel_id=1, source_target_pairs={{8,0},{12,4},{16,8},{20,12},{24,16},{28,20},{9,1},{13,5},{17,9},{2... | collective-permute-start | bytes 49160 | tf_op jit(solution)/shard_map/ppermute | solution.py:12
where the time goes:
time: 184 us
  other arithmetic  133 us (72%)
  blocking collectives  19.4 us (11%)
  local copies, waits for them, and re-layouts  17.8 us (10%)
  starting transfers between devices  12 us (7%)
    scatter-add x1, other arithmetic, on_device(): jnp.zeros((coef_share, span), jnp.float32).at[:, wide_index]  132 us
    ppermute x4, starting transfers between devices, passed_along(): lax.ppermute(value, axis, [(source, source + steps) for source in range(f...  12 us
    psum x1, blocking collectives, on_device(): potential = lax.psum(partial_sum, 'coef')  7.78 us
    reshape x1, local copies, waits for them, and re-layouts, on_device(): flat_terms = translated.reshape(coef_share, -1)  7.75 us
    all_gather x1, blocking collectives, on_device(): lax.all_gather(multipole, 'coef', axis=0, tiled=True)  6.42 us
    gather x2, local copies, waits for them, and re-layouts, on_device(): columns = leaf_local[:, leaf_index]  5.77 us
    all_gather x1, blocking collectives, on_device(): lax.all_gather(parent_local, 'coef', axis=0, tiled=True)  5.21 us
    unnamed x13, local copies, waits for them, and re-layouts  4.27 us
  transfers between devices with their start and end apart: 4, of which 0 were waited for; matrix products, arithmetic and copies ran while one was open for 0% of the time, Pallas kernels for 0%

commit v1 on v0

v1 whole, which is shorter than its diff:
```python
import functools

import jax
import jax.numpy as jnp
from jax import lax
from jax.experimental import pallas as pl
from jax.experimental.pallas import tpu as pltpu
from jax.sharding import PartitionSpec as P

REACH = 2
BLOCKS = 2 * REACH + 1
GROUP = 8


def far_kernel(ops_ref, full_ref, tgt_ref, l2l_ref, *refs, share, cells, parents, noff):
    outs = refs[:BLOCKS]
    poles_t, hot, rhs, acc = refs[BLOCKS:]
    f32, bf16 = jnp.float32, jnp.bfloat16
    lanes = 4 * share
    poles_t[...] = full_ref[:, :cells].astype(f32).T.astype(bf16)
    acc[...] = jnp.zeros_like(acc)
    rows = lax.broadcasted_iota(jnp.int32, (cells, cells), 0).astype(f32).astype(bf16)
    lane = lax.broadcasted_iota(jnp.int32, (cells, lanes), 1)
    is_high = (lane % (2 * share)) < share
    is_even = lane < 2 * share
    one = jnp.ones((cells, cells), bf16)
    zero = jnp.zeros((cells, cells), bf16)

    def chunk(first, count):
        wide = tgt_ref[pl.ds(first, count), :]
        for b in range(BLOCKS):
            local = jnp.clip(wide - b * cells, -1, cells).astype(f32)
            for j in range(count):
                row = jnp.broadcast_to(local[j : j + 1, :], (cells, cells)).astype(bf16)
                hot[b * cells : (b + 1) * cells, j * cells : (j + 1) * cells] = jnp.where(
                    row == rows, one, zero
                )
        for j in range(0, count, 2):
            pair = min(2, count - j)
            parts = []
            for i in range(2):
                op = ops_ref[first + j + min(i, pair - 1)]
                parts += [op, op]
            weights = jnp.concatenate(parts, axis=0)
            term = lax.dot_general(
                poles_t[...], weights, (((1,), (1,)), ((), ())), preferred_element_type=f32
            )
            high = term.astype(bf16).astype(f32)
            both = jnp.where(is_high, high, term - high)
            rhs[j * cells : (j + 1) * cells, :] = jnp.where(is_even, both, 0.0).astype(bf16)
            if pair == 2:
                rhs[(j + 1) * cells : (j + 2) * cells, :] = jnp.where(is_even, 0.0, both).astype(bf16)
        width = count * cells
        acc[...] += jnp.dot(hot[:, :width], rhs[:width, :], preferred_element_type=f32)

    whole = noff // GROUP

    def step(i, carry):
        chunk(pl.multiple_of(i * GROUP, GROUP), GROUP)
        return carry

    lax.fori_loop(0, whole, step, 0)
    if noff % GROUP:
        chunk(whole * GROUP, noff % GROUP)

    parent = full_ref[:, cells:]
    width = parent.shape[1]
    src = lax.broadcasted_iota(jnp.int32, (width, cells), 0)
    dst = lax.broadcasted_iota(jnp.int32, (width, cells), 1)
    children = cells // parents
    spread = jnp.where(dst // children == src, 1.0, 0.0).astype(bf16)
    rep = jnp.dot(parent, spread, preferred_element_type=f32)
    octant = lax.broadcasted_iota(jnp.int32, rep.shape, 1) % children
    shifted = jnp.zeros((share, cells), f32)
    for o in range(children):
        chosen = jnp.where(octant == o, rep, 0.0).astype(bf16)
        shifted = shifted + jnp.dot(l2l_ref[o], chosen, preferred_element_type=f32)

    for b in range(BLOCKS):
        t = acc[b * cells : (b + 1) * cells, :].T
        t = (t[:share] + t[share : 2 * share]) + (t[2 * share : 3 * share] + t[3 * share :])
        outs[b][...] = t + shifted if b == REACH else t


def near_kernel(*refs, share, cells):
    pieces = refs[:BLOCKS]
    leaf_ref, basis_ref, out_ref, pot_ref = refs[BLOCKS:]
    f32, bf16 = jnp.float32, jnp.bfloat16
    leaf = pieces[0][...]
    for piece in pieces[1:]:
        leaf = leaf + piece[...]
    out_ref[...] = leaf
    high = leaf.astype(bf16)
    low = (leaf - high.astype(f32)).astype(bf16)
    both = jnp.concatenate([high, low], axis=0)
    count = leaf_ref.shape[1]
    rows = lax.broadcasted_iota(jnp.int32, (cells, count), 0)
    hot = jnp.where(rows == leaf_ref[...], 1.0, 0.0).astype(bf16)
    columns = jnp.dot(both, hot, preferred_element_type=f32)
    columns = columns[:share] + columns[share:]
    pot_ref[...] = jnp.sum(columns * basis_ref[...].astype(f32), axis=0, keepdims=True)


def passed_along(value, axis, steps):
    count = lax.axis_size(axis)
    first, last = (max(0, -steps), min(count, count - steps))
    return lax.ppermute(value, axis, [(source, source + steps) for source in range(first, last)])


def on_device(
    multipole, parent_local, m2l_ops, l2l_ops, target_cell, particle_leaf, particle_basis
):
    my_index = lax.axis_index("cells")
    cells = multipole.shape[1]
    parents = parent_local.shape[1]
    noff, share, width = m2l_ops.shape
    pad = -parents % 128
    joined = jnp.concatenate(
        [multipole, parent_local, jnp.zeros((multipole.shape[0], pad), multipole.dtype)], axis=1
    )
    full = lax.all_gather(joined, "coef", axis=0, tiled=True)
    span = BLOCKS * cells
    lowest = (my_index - REACH) * cells
    wide = jnp.where(target_cell >= 0, target_cell - lowest, span)
    vmem = pl.BlockSpec(memory_space=pltpu.VMEM)
    blocks = pl.pallas_call(
        functools.partial(far_kernel, share=share, cells=cells, parents=parents, noff=noff),
        out_shape=[jax.ShapeDtypeStruct((share, cells), jnp.float32)] * BLOCKS,
        in_specs=[vmem] * 4,
        out_specs=[vmem] * BLOCKS,
        scratch_shapes=[
            pltpu.VMEM((cells, width), jnp.bfloat16),
            pltpu.VMEM((span, GROUP * cells), jnp.bfloat16),
            pltpu.VMEM((GROUP * cells, 4 * share), jnp.bfloat16),
            pltpu.VMEM((span, 4 * share), jnp.float32),
        ],
        name="far",
    )(m2l_ops, full, wide, l2l_ops)
    pieces = [blocks[REACH]]
    for length in range(1, REACH + 1):
        for direction in (1, -1):
            distance = length * direction
            pieces.append(passed_along(blocks[REACH + distance], "cells", distance))
    index = (particle_leaf - my_index * cells).reshape(1, -1)
    count = index.shape[1]
    leaf_local, partial = pl.pallas_call(
        functools.partial(near_kernel, share=share, cells=cells),
        out_shape=[
            jax.ShapeDtypeStruct((share, cells), jnp.float32),
            jax.ShapeDtypeStruct((1, count), jnp.float32),
        ],
        in_specs=[vmem] * (BLOCKS + 2),
        out_specs=[vmem] * 2,
        name="near",
    )(*pieces, index, particle_basis)
    potential = lax.psum(partial.reshape(-1), "coef")
    return (leaf_local, potential)


def solution(mesh):
    return jax.shard_map(
        on_device,
        mesh=mesh,
        in_specs=(
            P("coef", "cells"),
            P("coef", "cells"),
            P(None, "coef", None),
            P(None, "coef", None),
            P(None, "cells"),
            P("cells"),
            P("coef", "cells"),
        ),
        out_specs=(P("coef", "cells"), P("cells")),
        check_vma=False,
    )
```

time: 184 us -> 55.4 us (0.30)
  other arithmetic: 133 us -> 2.84 us
  Pallas kernels: 0 us -> 21 us
  local copies, waits for them, and re-layouts: 17.8 us -> 1.46 us
  blocking collectives: 19.4 us -> 13.1 us
  waiting for transfers between devices: 0.01 us -> 3.89 us
    scatter-add x1 -> x0, other arithmetic: 132 us -> none  [on_device(): jnp.zeros((coef_share, span), jnp.float32).at[:, wide_index]]
    pallas_call x0 -> x2, Pallas kernels: none -> 21 us  [the longest x1 19.2 us: on_device(): pl.pallas_call(functools.partial(far_kernel, share=share, cells=cells, pa...]
    reshape x1 -> x0, local copies, waits for them, and re-layouts: 7.75 us -> none  [on_device(): flat_terms = translated.reshape(coef_share, -1)]
    gather x2 -> x0, local copies, waits for them, and re-layouts: 5.77 us -> none  [on_device(): columns = leaf_local[:, leaf_index]]
    all_gather x2 -> x1, blocking collectives: 11.6 us -> 6.62 us  [on_device(): full = lax.all_gather(joined, 'coef', axis=0, tiled=True)]
    ppermute x4, waiting for transfers between devices: 0.01 us -> 3.89 us  [passed_along(): lax.ppermute(value, axis, [(source, source + steps) for source in range(f...]
    unnamed x13 -> x11, local copies, waits for them, and re-layouts: 4.27 us -> 1.37 us
  transfers between devices with their start and end apart: 4 -> 4, of which waited for: 0 -> 1; matrix products, arithmetic and copies ran while one was open for 0% -> 1% of each run, Pallas kernels for 0% -> 0%
where the time goes in v1:
time: 55.4 us; the launch traced here: 55 us
  Pallas kernels  21 us (38%)
  blocking collectives  13.1 us (24%)
  starting transfers between devices  12 us (22%)
  waiting for transfers between devices  3.89 us (7%)
  other arithmetic  2.84 us (5%)
  local copies, waits for them, and re-layouts  1.46 us (3%)
  between operations  0.72 us (1%)
    pallas_call x1, Pallas kernels, on_device(): pl.pallas_call(functools.partial(far_kernel, share=share, cells=cells, pa...  19.2 us
    ppermute x4, starting transfers between devices, passed_along(): lax.ppermute(value, axis, [(source, source + steps) for source in range(f...  12 us
    all_gather x1, blocking collectives, on_device(): full = lax.all_gather(joined, 'coef', axis=0, tiled=True)  6.62 us
    psum x1, blocking collectives, on_device(): potential = lax.psum(partial.reshape(-1), 'coef')  6.44 us
    ppermute x4, waiting for transfers between devices, passed_along(): lax.ppermute(value, axis, [(source, source + steps) for source in range(f...  3.89 us
    pallas_call x1, Pallas kernels, on_device(): pl.pallas_call(functools.partial(near_kernel, share=share, cells=cells),...  1.84 us
    select_n x1, other arithmetic, on_device(): wide = jnp.where(target_cell >= 0, target_cell - lowest, span)  1.54 us
    unnamed x11, local copies, waits for them, and re-layouts  1.37 us
  transfers between devices with their start and end apart: 4, of which 1 were waited for; matrix products, arithmetic and copies ran while one was open for 1% of the time, Pallas kernels for 0%

profile of v1, /device:TPU:0, one launch (start us, length us, event | category | flops | bytes accessed | tf_op | source)
XLA Modules:
  0.0 55.0 jit_solution(14382255069038165654)
XLA Ops:
  0.6 0.0 copy-start.4
  0.6 0.8 %copy.9 = bf16[32,16]{1,0:T(8,128)(2,1)S(1)} copy(bf16[32,16]{0,1:T(8,128)(2,1)} %param.8) | data formatting | bytes 2048 | tf_op args[1]
  1.4 0.1 pad.2.clone
  1.5 0.7 %maximum_maximum_fusion = bf16[32,256]{1,0:T(8,128)(2,1)S(1)} fusion(bf16[32,16]{1,0:T(8,128)(2,1)S(1)} %copy.9, bf16[32,128]{1,0:T(8,128)(2,1)} %param.7, bf16[256]{0:T(256)(128)(2,1)S(1)} %pad.2.clone), kind=kLoop, calls=%fused_computation.1 | loop fusion | flops 49152 | bytes 26112 | tf_op jit(solution)/shard_map/concatenate | solution.py:118
  2.2 6.6 %all_gather.3.full_ref = bf16[128,256]{1,0:T(8,128)(2,1)} all-gather(bf16[32,256]{1,0:T(8,128)(2,1)S(1)} %maximum_maximum_fusion), channel_id=1, replica_groups=mesh['cells'=8,'coef'=4] {'coef'}, dimensions={0}, use_global_device_ids=true | all-gather | bytes 81920 | tf_op jit(solution)/shard_map/all_gather | solution.py:121
  8.8 1.5 %subtract_select_fusion.tgt_ref = s32[189,128]{1,0:T(8,128)} fusion(s32[189,128]{1,0:T(8,128)} %param.11, s32[]{:T(128)S(6)} %mul.6), kind=kLoop, calls=%fused_computation | loop fusion | flops 72576 | bytes 193540 | tf_op jit(solution)/shard_map/jit(_where)/select_n | solution.py:124
  10.4 19.2 %far.1 = (f32[32,128]{1,0:T(8,128)}, f32[32,128]{1,0:T(8,128)}, f32[32,128]{1,0:T(8,128)}, f32[32,128]{1,0:T(8,128)}, f32[32,128]{1,0:T(8,128)}) custom-call(bf16[189,32,128]{2,1,0:T(8,128)(2,1)} %ops_ref.1, bf16[128,256]{1,0:T(8,128)(2,1)} %all_gather.3.full_ref, s32[189,128]{1,0:T(8,128)} %subtract_select_fusion.tgt_ref, bf16[8,32,128]{2,1,0:T(8,128)(2,1)} %l2l_ref.1), custom_call_target="tpu_custom_call" | custom-call | tf_op jit(solution)/shard_map/far/pallas_call | solution.py:126
  29.5 3.9 %collective-permute-start = (f32[32,128]{1,0:T(8,128)}, f32[32,128]{1,0:T(8,128)S(1)}, u32[]{:S(2)}, u32[]{:S(2)}) collective-permute-start(f32[32,128]{1,0:T(8,128)} %get-tuple-element.10), channel_id=1, source_target_pairs={{0,4},{4,8},{8,12},{12,16},{16,20},{20,24},{24,28},{1,5},{5,9},{9,... | collective-permute-start | bytes 49160 | tf_op jit(solution)/shard_map/ppermute | solution.py:107
  33.5 1.3 %collective-permute-start.1 = (f32[32,128]{1,0:T(8,128)}, f32[32,128]{1,0:T(8,128)S(1)}, u32[]{:S(2)}, u32[]{:S(2)}) collective-permute-start(f32[32,128]{1,0:T(8,128)} %get-tuple-element.11), channel_id=1, source_target_pairs={{4,0},{8,4},{12,8},{16,12},{20,16},{24,20},{28,24},{5,1},{9,5},{13... | collective-permute-start | bytes 49160 | tf_op jit(solution)/shard_map/ppermute | solution.py:107
  34.8 5.5 %collective-permute-start.2 = (f32[32,128]{1,0:T(8,128)}, f32[32,128]{1,0:T(8,128)S(1)}, u32[]{:S(2)}, u32[]{:S(2)}) collective-permute-start(f32[32,128]{1,0:T(8,128)} %get-tuple-element.12), channel_id=1, source_target_pairs={{0,8},{4,12},{8,16},{12,20},{16,24},{20,28},{1,9},{5,13},{9,17},{1... | collective-permute-start | bytes 49160 | tf_op jit(solution)/shard_map/ppermute | solution.py:107
  40.3 1.3 %collective-permute-start.3 = (f32[32,128]{1,0:T(8,128)}, f32[32,128]{1,0:T(8,128)S(1)}, u32[]{:S(2)}, u32[]{:S(2)}) collective-permute-start(f32[32,128]{1,0:T(8,128)} %get-tuple-element.13), channel_id=1, source_target_pairs={{8,0},{12,4},{16,8},{20,12},{24,16},{28,20},{9,1},{13,5},{17,9},{2... | collective-permute-start | bytes 49160 | tf_op jit(solution)/shard_map/ppermute | solution.py:107
  41.6 0.0 copy-done.4
  41.6 0.6 %broadcast_subtract_fusion = s32[2048]{0:T(1024)} fusion(s32[2048]{0:T(1024)S(1)} %copy-done.4, s32[]{:T(128)S(6)} %mul.7), kind=kLoop, calls=%fused_computation.2 | loop fusion | flops 2048 | bytes 16388 | tf_op jit(solution)/shard_map/sub | solution.py:144
  42.2 0.0 collective-permute-done.refs_1_
  42.2 0.0 copy-start
  42.2 0.0 collective-permute-done.1.refs_2_
  42.2 0.0 copy-start.1
  42.2 0.0 collective-permute-done.2.refs_3_
  42.2 0.0 copy-start.2
  42.2 3.9 %collective-permute-done.3.refs_4_ = f32[32,128]{1,0:T(8,128)S(1)} collective-permute-done((f32[32,128]{1,0:T(8,128)}, f32[32,128]{1,0:T(8,128)S(1)}, u32[]{:S(2)}, u32[]{:S(2)}) %collective-permute-start.3) | collective-permute-done | bytes 16416 | tf_op jit(solution)/shard_map/ppermute | solution.py:107
  46.1 0.0 copy-start.3
  46.1 0.0 copy-done
  46.1 0.0 copy-done.1
  46.1 0.0 copy-done.2
  46.1 0.6 %copy-done.3 = f32[32,128]{1,0:T(8,128)} copy-done((f32[32,128]{1,0:T(8,128)}, f32[32,128]{1,0:T(8,128)S(1)}, u32[]{:S(2)}) %copy-start.3) | copy-done | bytes 16408
  46.7 1.8 %near.1 = (f32[32,128]{1,0:T(8,128)}, f32[1,2048]{1,0:T(1,128)}) custom-call(f32[32,128]{1,0:T(8,128)} %get-tuple-element.9.refs_0_, f32[32,128]{1,0:T(8,128)} %copy-done, f32[32,128]{1,0:T(8,128)} %copy-done.1, f32[32,128]{1,0:T(8,128)} %copy-done.2, f32[32,128]{1,0:T(8,128)} %copy-done.3, s32[1,2048]{1,0:T(1,128)} %bitcast.2, bf16[32,2048]{1,0:T(8,128)(2,1)} %refs_6_.1), custom_call_target="tpu_custom_call" | custom-call | tf_op jit(solution)/shard_map/near/pallas_call | solution.py:146
  48.6 6.4 %psum.7 = f32[2048]{0:T(1024)} all-reduce(f32[2048]{0:T(1024)} %bitcast.3), channel_id=1, replica_groups=mesh['cells'=8,'coef'=4] {'coef'}, use_global_device_ids=true, to_apply=%region_0.1 | all-reduce | flops 2048 | bytes 16384 | tf_op jit(solution)/shard_map/psum | solution.py:156
  (1 shorter events, 0.0 us)
Async XLA Ops:
  0.6 40.9 %copy-start.4 = (s32[2048]{0:T(1024)S(1)}, s32[2048]{0:T(1024)}, u32[]{:S(2)}) copy-start(s32[2048]{0:T(1024)} %param.12) | copy-start | bytes 24580
  29.5 12.7 %collective-permute-start = (f32[32,128]{1,0:T(8,128)}, f32[32,128]{1,0:T(8,128)S(1)}, u32[]{:S(2)}, u32[]{:S(2)}) collective-permute-start(f32[32,128]{1,0:T(8,128)} %get-tuple-element.10), channel_id=1, source_target_pairs={{0,4},{4,8},{8,12},{12,16},{16,20},{20,24},{24,28},{1,5},{5,9},{9,... | collective-permute-start | bytes 49160 | tf_op jit(solution)/shard_map/ppermute | solution.py:107
  33.5 8.7 %collective-permute-start.1 = (f32[32,128]{1,0:T(8,128)}, f32[32,128]{1,0:T(8,128)S(1)}, u32[]{:S(2)}, u32[]{:S(2)}) collective-permute-start(f32[32,128]{1,0:T(8,128)} %get-tuple-element.11), channel_id=1, source_target_pairs={{4,0},{8,4},{12,8},{16,12},{20,16},{24,20},{28,24},{5,1},{9,5},{13... | collective-permute-start | bytes 49160 | tf_op jit(solution)/shard_map/ppermute | solution.py:107
  34.8 7.4 %collective-permute-start.2 = (f32[32,128]{1,0:T(8,128)}, f32[32,128]{1,0:T(8,128)S(1)}, u32[]{:S(2)}, u32[]{:S(2)}) collective-permute-start(f32[32,128]{1,0:T(8,128)} %get-tuple-element.12), channel_id=1, source_target_pairs={{0,8},{4,12},{8,16},{12,20},{16,24},{20,28},{1,9},{5,13},{9,17},{1... | collective-permute-start | bytes 49160 | tf_op jit(solution)/shard_map/ppermute | solution.py:107
  40.3 5.8 %collective-permute-start.3 = (f32[32,128]{1,0:T(8,128)}, f32[32,128]{1,0:T(8,128)S(1)}, u32[]{:S(2)}, u32[]{:S(2)}) collective-permute-start(f32[32,128]{1,0:T(8,128)} %get-tuple-element.13), channel_id=1, source_target_pairs={{8,0},{12,4},{16,8},{20,12},{24,16},{28,20},{9,1},{13,5},{17,9},{2... | collective-permute-start | bytes 49160 | tf_op jit(solution)/shard_map/ppermute | solution.py:107
  42.2 3.9 %copy-start = (f32[32,128]{1,0:T(8,128)}, f32[32,128]{1,0:T(8,128)S(1)}, u32[]{:S(2)}) copy-start(f32[32,128]{1,0:T(8,128)S(1)} %collective-permute-done.refs_1_) | copy-start | bytes 49156
  42.2 3.9 %copy-start.1 = (f32[32,128]{1,0:T(8,128)}, f32[32,128]{1,0:T(8,128)S(1)}, u32[]{:S(2)}) copy-start(f32[32,128]{1,0:T(8,128)S(1)} %collective-permute-done.1.refs_2_) | copy-start | bytes 49156
  42.2 3.9 %copy-start.2 = (f32[32,128]{1,0:T(8,128)}, f32[32,128]{1,0:T(8,128)S(1)}, u32[]{:S(2)}) copy-start(f32[32,128]{1,0:T(8,128)S(1)} %collective-permute-done.2.refs_3_) | copy-start | bytes 49156
  46.1 0.6 %copy-start.3 = (f32[32,128]{1,0:T(8,128)}, f32[32,128]{1,0:T(8,128)S(1)}, u32[]{:S(2)}) copy-start(f32[32,128]{1,0:T(8,128)S(1)} %collective-permute-done.3.refs_4_) | copy-start | bytes 49156

commit v2 on v1

--- a/solution.py
+++ b/solution.py
@@ -12,12 +12,36 @@
 GROUP = 8
 
 
-def far_kernel(ops_ref, full_ref, tgt_ref, l2l_ref, *refs, share, cells, parents, noff):
-    outs = refs[:BLOCKS]
-    poles_t, hot, rhs, acc = refs[BLOCKS:]
+def swap_steps(index):
+    steps = []
+    for length in range(1, REACH + 1):
+        side = (index // length) % 2
+        steps += [length * (1 - 2 * side), length * (2 * side - 1)]
+    return steps
+
+
+def far_kernel(*refs, share, cells, parents, noff, coefs):
     f32, bf16 = jnp.float32, jnp.bfloat16
+    shards = refs[:coefs]
+    ops_ref, tgt_ref, l2l_ref = refs[coefs : coefs + 3]
+    outs = refs[coefs + 3 : coefs + 3 + BLOCKS]
+    poles, spread_parents, poles_t, hot, rhs, acc = refs[coefs + 3 + BLOCKS :]
+    cell_index = lax.axis_index("cells")
+    coef_index = lax.axis_index("coef")
+    lowest = (cell_index - REACH) * cells
     lanes = 4 * share
-    poles_t[...] = full_ref[:, :cells].astype(f32).T.astype(bf16)
+    children = cells // parents
+    src = lax.broadcasted_iota(jnp.int32, (parents, cells), 0)
+    dst = lax.broadcasted_iota(jnp.int32, (parents, cells), 1)
+    spread = jnp.where(dst // children == src, 1.0, 0.0).astype(bf16)
+    for k in range(coefs):
+        at = pl.multiple_of((coef_index ^ k) * share, share)
+        shard = shards[k][...]
+        poles[pl.ds(at, share), :] = shard[:share, :]
+        spread_parents[pl.ds(at, share), :] = lax.dot_general(
+            shard[share:, :], spread, (((0,), (0,)), ((), ())), preferred_element_type=f32
+        )[:share]
+    poles_t[...] = poles[...].astype(f32).T.astype(bf16)
     acc[...] = jnp.zeros_like(acc)
     rows = lax.broadcasted_iota(jnp.int32, (cells, cells), 0).astype(f32).astype(bf16)
     lane = lax.broadcasted_iota(jnp.int32, (cells, lanes), 1)
@@ -27,7 +51,8 @@
     zero = jnp.zeros((cells, cells), bf16)
 
     def chunk(first, count):
-        wide = tgt_ref[pl.ds(first, count), :]
+        target = tgt_ref[pl.ds(first, count), :]
+        wide = jnp.where(target >= 0, target - lowest, -1)
         for b in range(BLOCKS):
             local = jnp.clip(wide - b * cells, -1, cells).astype(f32)
             for j in range(count):
@@ -63,23 +88,19 @@
     if noff % GROUP:
         chunk(whole * GROUP, noff % GROUP)
 
-    parent = full_ref[:, cells:]
-    width = parent.shape[1]
-    src = lax.broadcasted_iota(jnp.int32, (width, cells), 0)
-    dst = lax.broadcasted_iota(jnp.int32, (width, cells), 1)
-    children = cells // parents
-    spread = jnp.where(dst // children == src, 1.0, 0.0).astype(bf16)
-    rep = jnp.dot(parent, spread, preferred_element_type=f32)
+    rep = spread_parents[...]
     octant = lax.broadcasted_iota(jnp.int32, rep.shape, 1) % children
     shifted = jnp.zeros((share, cells), f32)
     for o in range(children):
         chosen = jnp.where(octant == o, rep, 0.0).astype(bf16)
         shifted = shifted + jnp.dot(l2l_ref[o], chosen, preferred_element_type=f32)
 
-    for b in range(BLOCKS):
-        t = acc[b * cells : (b + 1) * cells, :].T
+    steps = [0] + swap_steps(cell_index)
+    for out, step in zip(outs, steps):
+        at = pl.multiple_of((REACH + step) * cells, cells)
+        t = acc[pl.ds(at, cells), :].T
         t = (t[:share] + t[share : 2 * share]) + (t[2 * share : 3 * share] + t[3 * share :])
-        outs[b][...] = t + shifted if b == REACH else t
+        out[...] = t if out is not outs[0] else t + shifted
 
 
 def near_kernel(*refs, share, cells):
@@ -101,10 +122,20 @@
     pot_ref[...] = jnp.sum(columns * basis_ref[...].astype(f32), axis=0, keepdims=True)
 
 
-def passed_along(value, axis, steps):
-    count = lax.axis_size(axis)
-    first, last = (max(0, -steps), min(count, count - steps))
-    return lax.ppermute(value, axis, [(source, source + steps) for source in range(first, last)])
+def swapped(value, length, phase):
+    count = lax.axis_size("cells")
+    pairs = []
+    for low in range(count - length):
+        if (low // length) % 2 == phase:
+            pairs += [(low, low + length), (low + length, low)]
+    return lax.ppermute(value, "cells", pairs)
+
+
+def from_all(value):
+    count = lax.axis_size("coef")
+    return [value] + [
+        lax.ppermute(value, "coef", [(i, i ^ k) for i in range(count)]) for k in range(1, count)
+    ]
 
 
 def on_device(
@@ -113,34 +144,33 @@
     my_index = lax.axis_index("cells")
     cells = multipole.shape[1]
     parents = parent_local.shape[1]
+    coefs = lax.axis_size("coef")
     noff, share, width = m2l_ops.shape
-    pad = -parents % 128
-    joined = jnp.concatenate(
-        [multipole, parent_local, jnp.zeros((multipole.shape[0], pad), multipole.dtype)], axis=1
-    )
-    full = lax.all_gather(joined, "coef", axis=0, tiled=True)
+    flipped = jnp.pad(parent_local.T, ((0, 0), (0, cells - share)))
+    shards = from_all(jnp.concatenate([multipole, flipped], axis=0))
     span = BLOCKS * cells
-    lowest = (my_index - REACH) * cells
-    wide = jnp.where(target_cell >= 0, target_cell - lowest, span)
     vmem = pl.BlockSpec(memory_space=pltpu.VMEM)
     blocks = pl.pallas_call(
-        functools.partial(far_kernel, share=share, cells=cells, parents=parents, noff=noff),
+        functools.partial(
+            far_kernel, share=share, cells=cells, parents=parents, noff=noff, coefs=coefs
+        ),
         out_shape=[jax.ShapeDtypeStruct((share, cells), jnp.float32)] * BLOCKS,
-        in_specs=[vmem] * 4,
+        in_specs=[vmem] * (coefs + 3),
         out_specs=[vmem] * BLOCKS,
         scratch_shapes=[
+            pltpu.VMEM((width, cells), jnp.bfloat16),
+            pltpu.VMEM((width, cells), jnp.float32),
             pltpu.VMEM((cells, width), jnp.bfloat16),
             pltpu.VMEM((span, GROUP * cells), jnp.bfloat16),
             pltpu.VMEM((GROUP * cells, 4 * share), jnp.bfloat16),
             pltpu.VMEM((span, 4 * share), jnp.float32),
         ],
         name="far",
-    )(m2l_ops, full, wide, l2l_ops)
-    pieces = [blocks[REACH]]
+    )(*shards, m2l_ops, target_cell, l2l_ops)
+    pieces = [blocks[0]]
     for length in range(1, REACH + 1):
-        for direction in (1, -1):
-            distance = length * direction
-            pieces.append(passed_along(blocks[REACH + distance], "cells", distance))
+        for phase in range(2):
+            pieces.append(swapped(blocks[2 * length - 1 + phase], length, phase))
     index = (particle_leaf - my_index * cells).reshape(1, -1)
     count = index.shape[1]
     leaf_local, partial = pl.pallas_call(
@@ -153,8 +183,10 @@
         out_specs=[vmem] * 2,
         name="near",
     )(*pieces, index, particle_basis)
-    potential = lax.psum(partial.reshape(-1), "coef")
-    return (leaf_local, potential)
+    sums = from_all(partial.reshape(-1))
+    while len(sums) > 1:
+        sums = [a + b for a, b in zip(sums[::2], sums[1::2])]
+    return (leaf_local, sums[0])
 
 
 def solution(mesh):

time: 55.4 us -> 46.3 us (0.84)
  the two profiles are of different devices: /device:TPU:0 before, /device:TPU:13 now
where the time goes in v2:
time: 46.3 us; the launch traced here: 46 us
  Pallas kernels  21.2 us (46%)
  starting transfers between devices  14 us (30%)
  waiting for transfers between devices  6.22 us (13%)
  other arithmetic  2.63 us (6%)
  local copies, waits for them, and re-layouts  1.21 us (3%)
  between operations  0.72 us (2%)
    pallas_call x1, Pallas kernels, on_device(): pl.pallas_call(functools.partial(far_kernel, share=share, cells=cells, pa...  19.3 us
    ppermute x4, starting transfers between devices, swapped(): return lax.ppermute(value, 'cells', pairs)  7.66 us
    ppermute x6, starting transfers between devices, from_all(): lax.ppermute(value, 'coef', [(i, i ^ k) for i in range(count)])  6.35 us
    ppermute x6, waiting for transfers between devices, from_all(): lax.ppermute(value, 'coef', [(i, i ^ k) for i in range(count)])  5.24 us
    pallas_call x1, Pallas kernels, on_device(): pl.pallas_call(functools.partial(near_kernel, share=share, cells=cells),...  1.85 us
    add x1, other arithmetic, on_device(): sums = [a + b for a, b in zip(sums[::2], sums[1::2])]  1.3 us
    unnamed x18, local copies, waits for them, and re-layouts  1.21 us
    ppermute x4, waiting for transfers between devices, swapped(): return lax.ppermute(value, 'cells', pairs)  0.98 us
  transfers between devices with their start and end apart: 10, of which 5 were waited for; matrix products, arithmetic and copies ran while one was open for 1% of the time, Pallas kernels for 0%

profile of v2, /device:TPU:13, one launch (start us, length us, event | category | flops | bytes accessed | tf_op | source)
XLA Modules:
  0.0 46.0 jit_solution(8349754844916047975)
XLA Ops:
  0.6 0.0 copy-start.8
  0.6 0.7 %fusion.1.refs_0_ = bf16[48,128]{1,0:T(8,128)(2,1)S(1)} fusion(bf16[16,32]{1,0:T(8,128)(2,1)} %bitcast.8, bf16[32,128]{1,0:T(8,128)(2,1)} %param.7), kind=kLoop, calls=%fused_computation.2 | loop fusion | flops 36864 | bytes 21504 | tf_op jit(solution)/shard_map/concatenate | solution.py:150
  1.4 0.0 copy-start
  1.4 0.7 %collective-permute-start = (bf16[48,128]{1,0:T(8,128)(2,1)S(1)}, bf16[48,128]{1,0:T(8,128)(2,1)S(1)}, u32[]{:S(2)}, u32[]{:S(2)}) collective-permute-start(bf16[48,128]{1,0:T(8,128)(2,1)S(1)} %fusion.1.refs_0_), channel_id=1, source_target_pairs={{0,1},{1,0},{2,3},{3,2},{4,5},{5,4},{6,7},{7,6},{8,9},{9,8},{10,11... | collective-permute-start | bytes 36872 | tf_op jit(solution)/shard_map/ppermute | solution.py:137
  2.0 1.2 %collective-permute-start.1 = (bf16[48,128]{1,0:T(8,128)(2,1)S(1)}, bf16[48,128]{1,0:T(8,128)(2,1)S(1)}, u32[]{:S(2)}, u32[]{:S(2)}) collective-permute-start(bf16[48,128]{1,0:T(8,128)(2,1)S(1)} %fusion.1.refs_0_), channel_id=1, source_target_pairs={{0,2},{1,3},{2,0},{3,1},{4,6},{5,7},{6,4},{7,5},{8,10},{9,11},{10,... | collective-permute-start | bytes 36872 | tf_op jit(solution)/shard_map/ppermute | solution.py:137
  3.3 0.5 %collective-permute-start.2 = (bf16[48,128]{1,0:T(8,128)(2,1)S(1)}, bf16[48,128]{1,0:T(8,128)(2,1)S(1)}, u32[]{:S(2)}, u32[]{:S(2)}) collective-permute-start(bf16[48,128]{1,0:T(8,128)(2,1)S(1)} %fusion.1.refs_0_), channel_id=1, source_target_pairs={{0,3},{1,2},{2,1},{3,0},{4,7},{5,6},{6,5},{7,4},{8,11},{9,10},{10,... | collective-permute-start | bytes 36872 | tf_op jit(solution)/shard_map/ppermute | solution.py:137
  3.7 0.0 collective-permute-done.refs_1_
  3.7 0.0 copy-start.5
  3.7 0.8 %collective-permute-done.1.refs_2_ = bf16[48,128]{1,0:T(8,128)(2,1)S(1)} collective-permute-done((bf16[48,128]{1,0:T(8,128)(2,1)S(1)}, bf16[48,128]{1,0:T(8,128)(2,1)S(1)}, u32[]{:S(2)}, u32[]{:S(2)}) %collective-permute-start.1) | collective-permute-done | bytes 12320 | tf_op jit(solution)/shard_map/ppermute | solution.py:137
  4.6 0.0 copy-start.6
  4.6 1.8 %collective-permute-done.2.refs_3_ = bf16[48,128]{1,0:T(8,128)(2,1)S(1)} collective-permute-done((bf16[48,128]{1,0:T(8,128)(2,1)S(1)}, bf16[48,128]{1,0:T(8,128)(2,1)S(1)}, u32[]{:S(2)}, u32[]{:S(2)}) %collective-permute-start.2) | collective-permute-done | bytes 12320 | tf_op jit(solution)/shard_map/ppermute | solution.py:137
  6.4 0.0 copy-done
  6.4 0.0 copy-done.5
  6.4 0.0 copy-done.6
  6.4 0.0 copy-start.7
  6.4 0.6 %copy-done.7 = bf16[48,128]{1,0:T(8,128)(2,1)} copy-done((bf16[48,128]{1,0:T(8,128)(2,1)}, bf16[48,128]{1,0:T(8,128)(2,1)S(1)}, u32[]{:S(2)}) %copy-start.7) | copy-done | bytes 12312
  7.0 19.3 %far.1 = (f32[32,128]{1,0:T(8,128)}, f32[32,128]{1,0:T(8,128)}, f32[32,128]{1,0:T(8,128)}, f32[32,128]{1,0:T(8,128)}, f32[32,128]{1,0:T(8,128)}) custom-call(bf16[48,128]{1,0:T(8,128)(2,1)} %copy-done, bf16[48,128]{1,0:T(8,128)(2,1)} %copy-done.5, bf16[48,128]{1,0:T(8,128)(2,1)} %copy-done.6, bf16[48,128]{1,0:T(8,128)(2,1)} %copy-done.7, ...), custom_call_target="tpu_custom_call" | custom-call | tf_op jit(solution)/shard_map/far/pallas_call | solution.py:153
  26.3 0.2 collective-permute-start.3
  26.5 4.1 %collective-permute-start.4 = (f32[32,128]{1,0:T(8,128)}, f32[32,128]{1,0:T(8,128)S(1)}, u32[]{:S(2)}, u32[]{:S(2)}) collective-permute-start(f32[32,128]{1,0:T(8,128)} %get-tuple-element.11), channel_id=1, source_target_pairs={{4,8},{8,4},{12,16},{16,12},{20,24},{24,20},{5,9},{9,5},{13,17},{1... | collective-permute-start | bytes 49160 | tf_op jit(solution)/shard_map/ppermute | solution.py:131
  30.7 0.2 collective-permute-start.5
  30.9 3.0 %collective-permute-start.6 = (f32[32,128]{1,0:T(8,128)}, f32[32,128]{1,0:T(8,128)S(1)}, u32[]{:S(2)}, u32[]{:S(2)}) collective-permute-start(f32[32,128]{1,0:T(8,128)} %get-tuple-element.13), channel_id=1, source_target_pairs={{8,16},{16,8},{12,20},{20,12},{9,17},{17,9},{13,21},{21,13},{10,18... | collective-permute-start | bytes 49160 | tf_op jit(solution)/shard_map/ppermute | solution.py:131
  34.0 0.0 copy-done.8
  34.0 0.6 %broadcast_subtract_fusion = s32[2048]{0:T(1024)} fusion(s32[2048]{0:T(1024)S(1)} %copy-done.8, s32[]{:T(128)S(6)} %mul.3), kind=kLoop, calls=%fused_computation.4 | loop fusion | flops 2048 | bytes 16388 | tf_op jit(solution)/shard_map/sub | solution.py:174
  34.6 0.0 collective-permute-done.3.refs_1_
  34.6 0.0 copy-start.1
  34.6 0.0 collective-permute-done.4.refs_2_
  34.6 0.0 copy-start.2
  34.6 0.0 collective-permute-done.5.refs_3_
  34.6 0.0 copy-start.3
  34.6 1.0 %collective-permute-done.6.refs_4_ = f32[32,128]{1,0:T(8,128)S(1)} collective-permute-done((f32[32,128]{1,0:T(8,128)}, f32[32,128]{1,0:T(8,128)S(1)}, u32[]{:S(2)}, u32[]{:S(2)}) %collective-permute-start.6) | collective-permute-done | bytes 16416 | tf_op jit(solution)/shard_map/ppermute | solution.py:131
  35.6 0.0 copy-start.4
  35.6 0.0 copy-done.1
  35.6 0.0 copy-done.2
  35.6 0.0 copy-done.3
  35.6 0.6 %copy-done.4 = f32[32,128]{1,0:T(8,128)} copy-done((f32[32,128]{1,0:T(8,128)}, f32[32,128]{1,0:T(8,128)S(1)}, u32[]{:S(2)}) %copy-start.4) | copy-done | bytes 16408
  36.2 1.8 %near.1 = (f32[32,128]{1,0:T(8,128)}, f32[1,2048]{1,0:T(1,128)}) custom-call(f32[32,128]{1,0:T(8,128)} %get-tuple-element.9.refs_0_, f32[32,128]{1,0:T(8,128)} %copy-done.1, f32[32,128]{1,0:T(8,128)} %copy-done.2, f32[32,128]{1,0:T(8,128)} %copy-done.3, f32[32,128]{1,0:T(8,128)} %copy-done.4, s32[1,2048]{1,0:T(1,128)} %bitcast.3, bf16[32,2048]{1,0:T(8,128)(2,1)} %refs_6_.3), custom_call_target="tpu_custom_call" | custom-call | tf_op jit(solution)/shard_map/near/pallas_call | solution.py:176
  38.1 2.3 %collective-permute-start.7 = (f32[2048]{0:T(1024)}, f32[2048]{0:T(1024)S(1)}, u32[]{:S(2)}, u32[]{:S(2)}) collective-permute-start(f32[2048]{0:T(1024)} %bitcast.4), channel_id=1, source_target_pairs={{0,1},{1,0},{2,3},{3,2},{4,5},{5,4},{6,7},{7,6},{8,9},{9,8},{10,11... | collective-permute-start | bytes 24584 | tf_op jit(solution)/shard_map/ppermute | solution.py:137
  40.4 1.0 %collective-permute-start.8 = (f32[2048]{0:T(1024)}, f32[2048]{0:T(1024)S(1)}, u32[]{:S(2)}, u32[]{:S(2)}) collective-permute-start(f32[2048]{0:T(1024)} %bitcast.5), channel_id=1, source_target_pairs={{0,2},{1,3},{2,0},{3,1},{4,6},{5,7},{6,4},{7,5},{8,10},{9,11},{10,... | collective-permute-start | bytes 24584 | tf_op jit(solution)/shard_map/ppermute | solution.py:137
  41.4 0.7 %collective-permute-start.9 = (f32[2048]{0:T(1024)}, f32[2048]{0:T(1024)S(1)}, u32[]{:S(2)}, u32[]{:S(2)}) collective-permute-start(f32[2048]{0:T(1024)} %bitcast.6), channel_id=1, source_target_pairs={{0,3},{1,2},{2,1},{3,0},{4,7},{5,6},{6,5},{7,4},{8,11},{9,10},{10,... | collective-permute-start | bytes 24584 | tf_op jit(solution)/shard_map/ppermute | solution.py:137
  42.1 0.0 collective-permute-done.7
  42.1 1.1 %collective-permute-done.8 = f32[2048]{0:T(1024)S(1)} collective-permute-done((f32[2048]{0:T(1024)}, f32[2048]{0:T(1024)S(1)}, u32[]{:S(2)}, u32[]{:S(2)}) %collective-permute-start.8) | collective-permute-done | bytes 8224 | tf_op jit(solution)/shard_map/ppermute | solution.py:137
  43.1 1.5 %collective-permute-done.9 = f32[2048]{0:T(1024)S(1)} collective-permute-done((f32[2048]{0:T(1024)}, f32[2048]{0:T(1024)S(1)}, u32[]{:S(2)}, u32[]{:S(2)}) %collective-permute-start.9) | collective-permute-done | bytes 8224 | tf_op jit(solution)/shard_map/ppermute | solution.py:137
  44.7 1.3 %add_add_fusion = f32[2048]{0:T(1024)} fusion(f32[2048]{0:T(1024)S(1)} %collective-permute-done.8, f32[2048]{0:T(1024)S(1)} %collective-permute-done.9, f32[2048]{0:T(1024)} %bitcast.7, f32[2048]{0:T(1024)S(1)} %collective-permute-done.7), kind=kLoop, calls=%fused_computation.3 | loop fusion | flops 6144 | bytes 40960 | tf_op jit(solution)/shard_map/add | solution.py:188
Async XLA Ops:
  0.6 33.4 %copy-start.8 = (s32[2048]{0:T(1024)S(1)}, s32[2048]{0:T(1024)}, u32[]{:S(2)}) copy-start(s32[2048]{0:T(1024)} %param.12) | copy-start | bytes 24580
  1.4 5.0 %copy-start = (bf16[48,128]{1,0:T(8,128)(2,1)}, bf16[48,128]{1,0:T(8,128)(2,1)S(1)}, u32[]{:S(2)}) copy-start(bf16[48,128]{1,0:T(8,128)(2,1)S(1)} %fusion.1.refs_0_) | copy-start | bytes 36868
  1.4 2.4 %collective-permute-start = (bf16[48,128]{1,0:T(8,128)(2,1)S(1)}, bf16[48,128]{1,0:T(8,128)(2,1)S(1)}, u32[]{:S(2)}, u32[]{:S(2)}) collective-permute-start(bf16[48,128]{1,0:T(8,128)(2,1)S(1)} %fusion.1.refs_0_), channel_id=1, source_target_pairs={{0,1},{1,0},{2,3},{3,2},{4,5},{5,4},{6,7},{7,6},{8,9},{9,8},{10,11... | collective-permute-start | bytes 36872 | tf_op jit(solution)/shard_map/ppermute | solution.py:137
  2.0 2.5 %collective-permute-start.1 = (bf16[48,128]{1,0:T(8,128)(2,1)S(1)}, bf16[48,128]{1,0:T(8,128)(2,1)S(1)}, u32[]{:S(2)}, u32[]{:S(2)}) collective-permute-start(bf16[48,128]{1,0:T(8,128)(2,1)S(1)} %fusion.1.refs_0_), channel_id=1, source_target_pairs={{0,2},{1,3},{2,0},{3,1},{4,6},{5,7},{6,4},{7,5},{8,10},{9,11},{10,... | collective-permute-start | bytes 36872 | tf_op jit(solution)/shard_map/ppermute | solution.py:137
  3.3 3.1 %collective-permute-start.2 = (bf16[48,128]{1,0:T(8,128)(2,1)S(1)}, bf16[48,128]{1,0:T(8,128)(2,1)S(1)}, u32[]{:S(2)}, u32[]{:S(2)}) collective-permute-start(bf16[48,128]{1,0:T(8,128)(2,1)S(1)} %fusion.1.refs_0_), channel_id=1, source_target_pairs={{0,3},{1,2},{2,1},{3,0},{4,7},{5,6},{6,5},{7,4},{8,11},{9,10},{10,... | collective-permute-start | bytes 36872 | tf_op jit(solution)/shard_map/ppermute | solution.py:137
  3.7 2.6 %copy-start.5 = (bf16[48,128]{1,0:T(8,128)(2,1)}, bf16[48,128]{1,0:T(8,128)(2,1)S(1)}, u32[]{:S(2)}) copy-start(bf16[48,128]{1,0:T(8,128)(2,1)S(1)} %collective-permute-done.refs_1_) | copy-start | bytes 36868
  4.6 1.8 %copy-start.6 = (bf16[48,128]{1,0:T(8,128)(2,1)}, bf16[48,128]{1,0:T(8,128)(2,1)S(1)}, u32[]{:S(2)}) copy-start(bf16[48,128]{1,0:T(8,128)(2,1)S(1)} %collective-permute-done.1.refs_2_) | copy-start | bytes 36868
  6.4 0.6 %copy-start.7 = (bf16[48,128]{1,0:T(8,128)(2,1)}, bf16[48,128]{1,0:T(8,128)(2,1)S(1)}, u32[]{:S(2)}) copy-start(bf16[48,128]{1,0:T(8,128)(2,1)S(1)} %collective-permute-done.2.refs_3_) | copy-start | bytes 36868
  26.3 8.3 %collective-permute-start.3 = (f32[32,128]{1,0:T(8,128)}, f32[32,128]{1,0:T(8,128)S(1)}, u32[]{:S(2)}, u32[]{:S(2)}) collective-permute-start(f32[32,128]{1,0:T(8,128)} %get-tuple-element.10), channel_id=1, source_target_pairs={{0,4},{4,0},{8,12},{12,8},{16,20},{20,16},{24,28},{28,24},{1,5},{5... | collective-permute-start | bytes 49160 | tf_op jit(solution)/shard_map/ppermute | solution.py:131
  26.5 8.1 %collective-permute-start.4 = (f32[32,128]{1,0:T(8,128)}, f32[32,128]{1,0:T(8,128)S(1)}, u32[]{:S(2)}, u32[]{:S(2)}) collective-permute-start(f32[32,128]{1,0:T(8,128)} %get-tuple-element.11), channel_id=1, source_target_pairs={{4,8},{8,4},{12,16},{16,12},{20,24},{24,20},{5,9},{9,5},{13,17},{1... | collective-permute-start | bytes 49160 | tf_op jit(solution)/shard_map/ppermute | solution.py:131
  30.7 3.9 %collective-permute-start.5 = (f32[32,128]{1,0:T(8,128)}, f32[32,128]{1,0:T(8,128)S(1)}, u32[]{:S(2)}, u32[]{:S(2)}) collective-permute-start(f32[32,128]{1,0:T(8,128)} %get-tuple-element.12), channel_id=1, source_target_pairs={{0,8},{8,0},{4,12},{12,4},{16,24},{24,16},{20,28},{28,20},{1,9},{9... | collective-permute-start | bytes 49160 | tf_op jit(solution)/shard_map/ppermute | solution.py:131
  30.9 4.7 %collective-permute-start.6 = (f32[32,128]{1,0:T(8,128)}, f32[32,128]{1,0:T(8,128)S(1)}, u32[]{:S(2)}, u32[]{:S(2)}) collective-permute-start(f32[32,128]{1,0:T(8,128)} %get-tuple-element.13), channel_id=1, source_target_pairs={{8,16},{16,8},{12,20},{20,12},{9,17},{17,9},{13,21},{21,13},{10,18... | collective-permute-start | bytes 49160 | tf_op jit(solution)/shard_map/ppermute | solution.py:131
  34.6 1.0 %copy-start.1 = (f32[32,128]{1,0:T(8,128)}, f32[32,128]{1,0:T(8,128)S(1)}, u32[]{:S(2)}) copy-start(f32[32,128]{1,0:T(8,128)S(1)} %collective-permute-done.3.refs_1_) | copy-start | bytes 49156
  34.6 1.0 %copy-start.2 = (f32[32,128]{1,0:T(8,128)}, f32[32,128]{1,0:T(8,128)S(1)}, u32[]{:S(2)}) copy-start(f32[32,128]{1,0:T(8,128)S(1)} %collective-permute-done.4.refs_2_) | copy-start | bytes 49156
  34.6 1.0 %copy-start.3 = (f32[32,128]{1,0:T(8,128)}, f32[32,128]{1,0:T(8,128)S(1)}, u32[]{:S(2)}) copy-start(f32[32,128]{1,0:T(8,128)S(1)} %collective-permute-done.5.refs_3_) | copy-start | bytes 49156
  35.6 0.6 %copy-start.4 = (f32[32,128]{1,0:T(8,128)}, f32[32,128]{1,0:T(8,128)S(1)}, u32[]{:S(2)}) copy-start(f32[32,128]{1,0:T(8,128)S(1)} %collective-permute-done.6.refs_4_) | copy-start | bytes 49156
  38.1 4.0 %collective-permute-start.7 = (f32[2048]{0:T(1024)}, f32[2048]{0:T(1024)S(1)}, u32[]{:S(2)}, u32[]{:S(2)}) collective-permute-start(f32[2048]{0:T(1024)} %bitcast.4), channel_id=1, source_target_pairs={{0,1},{1,0},{2,3},{3,2},{4,5},{5,4},{6,7},{7,6},{8,9},{9,8},{10,11... | collective-permute-start | bytes 24584 | tf_op jit(solution)/shard_map/ppermute | solution.py:137
  40.4 2.7 %collective-permute-start.8 = (f32[2048]{0:T(1024)}, f32[2048]{0:T(1024)S(1)}, u32[]{:S(2)}, u32[]{:S(2)}) collective-permute-start(f32[2048]{0:T(1024)} %bitcast.5), channel_id=1, source_target_pairs={{0,2},{1,3},{2,0},{3,1},{4,6},{5,7},{6,4},{7,5},{8,10},{9,11},{10,... | collective-permute-start | bytes 24584 | tf_op jit(solution)/shard_map/ppermute | solution.py:137
  41.4 3.3 %collective-permute-start.9 = (f32[2048]{0:T(1024)}, f32[2048]{0:T(1024)S(1)}, u32[]{:S(2)}, u32[]{:S(2)}) collective-permute-start(f32[2048]{0:T(1024)} %bitcast.6), channel_id=1, source_target_pairs={{0,3},{1,2},{2,1},{3,0},{4,7},{5,6},{6,5},{7,4},{8,11},{9,10},{10,... | collective-permute-start | bytes 24584 | tf_op jit(solution)/shard_map/ppermute | solution.py:137

commit v3 on v2

--- a/solution.py
+++ b/solution.py
@@ -9,7 +9,9 @@
 
 REACH = 2
 BLOCKS = 2 * REACH + 1
-GROUP = 8
+GROUP = 32
+CAP = 256
+SLOTS = 2 * REACH * CAP
 
 
 def swap_steps(index):
@@ -20,20 +22,69 @@
     return steps
 
 
+def ones_where(mask):
+    return jnp.where(mask, 1.0, 0.0).astype(jnp.bfloat16)
+
+
+def plan_kernel(tgt_ref, row_ref, code_ref, total_ref, padded, *, cells, noff):
+    f32, bf16, i32 = jnp.float32, jnp.bfloat16, jnp.int32
+    rows = padded.shape[0]
+    padded[...] = jnp.full_like(padded, -1)
+    padded[:noff, :] = tgt_ref[...]
+    target = padded[...]
+    rel = target - (lax.axis_index("cells") - REACH) * cells
+    above = rel >= (REACH + 1) * cells
+    remote = (target >= 0) & ((rel < REACH * cells) | above)
+    code = jnp.where(above, rel - cells, rel)
+    iota = lambda shape, dim: lax.broadcasted_iota(i32, shape, dim)
+    mask = ones_where(remote)
+    before = ones_where(iota((cells, cells), 0) < iota((cells, cells), 1))
+    within = jnp.dot(mask, before, preferred_element_type=f32)
+    counts = jnp.dot(mask, jnp.ones((cells, cells), bf16), preferred_element_type=f32)
+    above_rows = ones_where(iota((rows, rows), 1) < iota((rows, rows), 0))
+    start = jnp.dot(above_rows, counts.astype(bf16), preferred_element_type=f32).astype(i32)
+    counts = counts.astype(i32)
+    rank = start + within.astype(i32)
+    high = jnp.where(remote, (rank >> 7) + 1, 0)
+    low = jnp.where(remote, rank & 127, 0)
+    block = jnp.where(remote, code // cells, 0)
+    local = jnp.where(remote, code % cells, 0)
+    data = jnp.concatenate([high, low, block, local], axis=1).astype(f32).astype(bf16)
+    lane = iota((rows, cells), 1)
+    offset = iota((rows, cells), 0).astype(f32)
+    for j in range(SLOTS // cells):
+        slot = lane + j * cells
+        hit = (start <= slot) & (slot < start + counts)
+        found = lax.dot_general(
+            data, ones_where(hit), (((0,), (0,)), ((), ())), preferred_element_type=f32
+        )
+        slot_c = iota((cells, cells), 1).astype(f32) + float(j * cells)
+        mine = found[:cells] * 128.0 + found[cells : 2 * cells] - 128.0 == slot_c
+        value = found[2 * cells : 3 * cells] * float(cells) + found[3 * cells :]
+        source = iota((cells, cells), 0).astype(f32)
+        code_s = jnp.sum(jnp.where(mine, value, 0.0), axis=0, keepdims=True).astype(i32)
+        cell_s = jnp.sum(jnp.where(mine, source, 0.0), axis=0, keepdims=True).astype(i32)
+        off_s = jnp.sum(jnp.where(hit, offset, 0.0), axis=0, keepdims=True).astype(i32)
+        used = jnp.sum(jnp.where(hit, 1.0, 0.0), axis=0, keepdims=True) > 0.0
+        at = slice(j * cells, (j + 1) * cells)
+        row_ref[:, at] = (off_s >> 1) * cells + cell_s
+        code_ref[:, at] = jnp.where(used, code_s + (off_s & 1) * (2 * REACH * cells), -1)
+    total_ref[...] = (start + counts)[rows - 8 :, :]
+
+
 def far_kernel(*refs, share, cells, parents, noff, coefs):
-    f32, bf16 = jnp.float32, jnp.bfloat16
+    f32, bf16, i32 = jnp.float32, jnp.bfloat16, jnp.int32
     shards = refs[:coefs]
-    ops_ref, tgt_ref, l2l_ref = refs[coefs : coefs + 3]
-    outs = refs[coefs + 3 : coefs + 3 + BLOCKS]
-    poles, spread_parents, poles_t, hot, rhs, acc = refs[coefs + 3 + BLOCKS :]
+    ops_ref, tgt_ref, l2l_ref, row_ref, code_ref, total_ref = refs[coefs : coefs + 6]
+    outs = refs[coefs + 6 : coefs + 6 + BLOCKS]
+    poles, spread_parents, poles_t, hot, rhs, acc, terms, picked, far = refs[coefs + 6 + BLOCKS :]
     cell_index = lax.axis_index("cells")
     coef_index = lax.axis_index("coef")
-    lowest = (cell_index - REACH) * cells
     lanes = 4 * share
     children = cells // parents
-    src = lax.broadcasted_iota(jnp.int32, (parents, cells), 0)
-    dst = lax.broadcasted_iota(jnp.int32, (parents, cells), 1)
-    spread = jnp.where(dst // children == src, 1.0, 0.0).astype(bf16)
+    src = lax.broadcasted_iota(i32, (parents, cells), 0)
+    dst = lax.broadcasted_iota(i32, (parents, cells), 1)
+    spread = ones_where(dst // children == src)
     for k in range(coefs):
         at = pl.multiple_of((coef_index ^ k) * share, share)
         shard = shards[k][...]
@@ -43,38 +94,45 @@
         )[:share]
     poles_t[...] = poles[...].astype(f32).T.astype(bf16)
     acc[...] = jnp.zeros_like(acc)
-    rows = lax.broadcasted_iota(jnp.int32, (cells, cells), 0).astype(f32).astype(bf16)
-    lane = lax.broadcasted_iota(jnp.int32, (cells, lanes), 1)
+    picked[...] = jnp.zeros_like(picked)
+    rows = lax.broadcasted_iota(i32, (cells, cells), 0).astype(f32).astype(bf16)
+    lane = lax.broadcasted_iota(i32, (cells, lanes), 1)
     is_high = (lane % (2 * share)) < share
     is_even = lane < 2 * share
     one = jnp.ones((cells, cells), bf16)
     zero = jnp.zeros((cells, cells), bf16)
 
     def chunk(first, count):
-        target = tgt_ref[pl.ds(first, count), :]
-        wide = jnp.where(target >= 0, target - lowest, -1)
-        for b in range(BLOCKS):
-            local = jnp.clip(wide - b * cells, -1, cells).astype(f32)
-            for j in range(count):
+        for base in range(0, count, 8):
+            size = min(8, count - base)
+            local = jnp.clip(tgt_ref[pl.ds(first + base, size), :] - cell_index * cells, -1, cells)
+            local = local.astype(f32)
+            for j in range(size):
                 row = jnp.broadcast_to(local[j : j + 1, :], (cells, cells)).astype(bf16)
-                hot[b * cells : (b + 1) * cells, j * cells : (j + 1) * cells] = jnp.where(
-                    row == rows, one, zero
-                )
-        for j in range(0, count, 2):
-            pair = min(2, count - j)
+                at = (base + j) * cells
+                hot[:, at : at + cells] = jnp.where(row == rows, one, zero)
+        for j in range(0, count, 4):
             parts = []
-            for i in range(2):
-                op = ops_ref[first + j + min(i, pair - 1)]
-                parts += [op, op]
-            weights = jnp.concatenate(parts, axis=0)
-            term = lax.dot_general(
-                poles_t[...], weights, (((1,), (1,)), ((), ())), preferred_element_type=f32
+            for i in range(0, min(4, count - j), 2):
+                even = ops_ref[first + j + i]
+                odd = ops_ref[first + j + i + 1] if j + i + 1 < count else even
+                parts += [even, even, odd, odd]
+            term4 = lax.dot_general(
+                poles_t[...],
+                jnp.concatenate(parts, axis=0),
+                (((1,), (1,)), ((), ())),
+                preferred_element_type=f32,
             )
-            high = term.astype(bf16).astype(f32)
-            both = jnp.where(is_high, high, term - high)
-            rhs[j * cells : (j + 1) * cells, :] = jnp.where(is_even, both, 0.0).astype(bf16)
-            if pair == 2:
-                rhs[(j + 1) * cells : (j + 2) * cells, :] = jnp.where(is_even, 0.0, both).astype(bf16)
+            for i in range(0, min(4, count - j), 2):
+                term = term4[:, i * 2 * share : i * 2 * share + lanes]
+                high = term.astype(bf16).astype(f32)
+                both = jnp.where(is_high, high, term - high)
+                at = pl.multiple_of((first + j + i) // 2 * cells, cells)
+                terms[pl.ds(at, cells), :] = both
+                at = (j + i) * cells
+                rhs[at : at + cells, :] = jnp.where(is_even, both, 0.0).astype(bf16)
+                if j + i + 1 < count:
+                    rhs[at + cells : at + 2 * cells, :] = jnp.where(is_even, 0.0, both).astype(bf16)
         width = count * cells
         acc[...] += jnp.dot(hot[:, :width], rhs[:width, :], preferred_element_type=f32)
 
@@ -88,19 +146,43 @@
     if noff % GROUP:
         chunk(whole * GROUP, noff % GROUP)
 
+    def pick(i, carry):
+        first = pl.multiple_of(i * 16, 16)
+        for j in range(16):
+            picked[pl.ds(first + j, 1), :] = terms[pl.ds(row_ref[0, first + j], 1), :]
+        return carry
+
+    lax.fori_loop(0, (total_ref[7, 0] + 15) // 16, pick, 0)
+
+    reach_cells = 2 * REACH * cells
+    target = lax.broadcasted_iota(i32, (2 * reach_cells, CAP), 0)
+    total = jnp.zeros((2 * reach_cells, lanes), f32)
+    for j in range(SLOTS // CAP):
+        at = slice(j * CAP, (j + 1) * CAP)
+        total = total + jnp.dot(
+            ones_where(code_ref[:, at] == target),
+            picked[at, :].astype(bf16),
+            preferred_element_type=f32,
+        )
+    even_lane = lax.broadcasted_iota(i32, (reach_cells, lanes), 1) < 2 * share
+    far[...] = jnp.where(even_lane, total[:reach_cells], total[reach_cells:])
+
     rep = spread_parents[...]
-    octant = lax.broadcasted_iota(jnp.int32, rep.shape, 1) % children
+    octant = lax.broadcasted_iota(i32, rep.shape, 1) % children
     shifted = jnp.zeros((share, cells), f32)
     for o in range(children):
         chosen = jnp.where(octant == o, rep, 0.0).astype(bf16)
         shifted = shifted + jnp.dot(l2l_ref[o], chosen, preferred_element_type=f32)
 
-    steps = [0] + swap_steps(cell_index)
-    for out, step in zip(outs, steps):
-        at = pl.multiple_of((REACH + step) * cells, cells)
-        t = acc[pl.ds(at, cells), :].T
-        t = (t[:share] + t[share : 2 * share]) + (t[2 * share : 3 * share] + t[3 * share :])
-        out[...] = t if out is not outs[0] else t + shifted
+    def folded(value):
+        t = value.T
+        return (t[:share] + t[share : 2 * share]) + (t[2 * share : 3 * share] + t[3 * share :])
+
+    outs[0][...] = folded(acc[...]) + shifted
+    for out, move in zip(outs[1:], swap_steps(cell_index)):
+        block = move + REACH - jnp.where(move > 0, 1, 0)
+        at = pl.multiple_of(block * cells, cells)
+        out[...] = folded(far[pl.ds(at, cells), :])
 
 
 def near_kernel(*refs, share, cells):
@@ -148,25 +230,42 @@
     noff, share, width = m2l_ops.shape
     flipped = jnp.pad(parent_local.T, ((0, 0), (0, cells - share)))
     shards = from_all(jnp.concatenate([multipole, flipped], axis=0))
-    span = BLOCKS * cells
     vmem = pl.BlockSpec(memory_space=pltpu.VMEM)
+    smem = pl.BlockSpec(memory_space=pltpu.SMEM)
+    i32 = jnp.int32
+    rows, codes, total = pl.pallas_call(
+        functools.partial(plan_kernel, cells=cells, noff=noff),
+        out_shape=[
+            jax.ShapeDtypeStruct((1, SLOTS), i32),
+            jax.ShapeDtypeStruct((1, SLOTS), i32),
+            jax.ShapeDtypeStruct((8, cells), i32),
+        ],
+        in_specs=[vmem],
+        out_specs=[vmem] * 3,
+        scratch_shapes=[pltpu.VMEM((noff + (-noff) % 16, cells), i32)],
+        name="plan",
+    )(target_cell)
+    lanes = 4 * share
     blocks = pl.pallas_call(
         functools.partial(
             far_kernel, share=share, cells=cells, parents=parents, noff=noff, coefs=coefs
         ),
         out_shape=[jax.ShapeDtypeStruct((share, cells), jnp.float32)] * BLOCKS,
-        in_specs=[vmem] * (coefs + 3),
+        in_specs=[vmem] * (coefs + 3) + [smem, vmem, smem],
         out_specs=[vmem] * BLOCKS,
         scratch_shapes=[
             pltpu.VMEM((width, cells), jnp.bfloat16),
             pltpu.VMEM((width, cells), jnp.float32),
             pltpu.VMEM((cells, width), jnp.bfloat16),
-            pltpu.VMEM((span, GROUP * cells), jnp.bfloat16),
-            pltpu.VMEM((GROUP * cells, 4 * share), jnp.bfloat16),
-            pltpu.VMEM((span, 4 * share), jnp.float32),
+            pltpu.VMEM((cells, GROUP * cells), jnp.bfloat16),
+            pltpu.VMEM((GROUP * cells, lanes), jnp.bfloat16),
+            pltpu.VMEM((cells, lanes), jnp.float32),
+            pltpu.VMEM(((noff + 1) // 2 * cells, lanes), jnp.float32),
+            pltpu.VMEM((SLOTS, lanes), jnp.float32),
+            pltpu.VMEM((2 * REACH * cells, lanes), jnp.float32),
         ],
         name="far",
-    )(*shards, m2l_ops, target_cell, l2l_ops)
+    )(*shards, m2l_ops, target_cell, l2l_ops, rows, codes, total)
     pieces = [blocks[0]]
     for length in range(1, REACH + 1):
         for phase in range(2):

time: 46.3 us -> 36.7 us (0.79)
  Pallas kernels: 21.2 us -> 14.2 us
  waiting for transfers between devices: 6.22 us -> 4.27 us
  starting transfers between devices: 14 us -> 13.4 us
    pallas_call x1, Pallas kernels: 19.3 us -> 9.58 us  [on_device(): pl.pallas_call(functools.partial(far_kernel, share=share, cells=cells, pa...]
    pallas_call x0 -> x1, Pallas kernels: none -> 2.75 us  [on_device(): pl.pallas_call(functools.partial(plan_kernel, cells=cells, noff=noff), ou...]
    ppermute x6, waiting for transfers between devices: 5.24 us -> 2.83 us  [from_all(): lax.ppermute(value, 'coef', [(i, i ^ k) for i in range(count)])]
    ppermute x4, starting transfers between devices: 7.66 us -> 7.19 us  [swapped(): return lax.ppermute(value, 'cells', pairs)]
    ppermute x4, waiting for transfers between devices: 0.98 us -> 1.44 us  [swapped(): return lax.ppermute(value, 'cells', pairs)]
  transfers between devices with their start and end apart: 10 -> 10, of which waited for: 5 -> 3; matrix products, arithmetic and copies ran while one was open for 1% -> 2% of each run, Pallas kernels for 0% -> 8%
where the time goes in v3:
time: 36.7 us; the launch traced here: 36.4 us
  Pallas kernels  14.2 us (39%)
  starting transfers between devices  13.4 us (37%)
  waiting for transfers between devices  4.27 us (12%)
  other arithmetic  2.63 us (7%)
  local copies, waits for them, and re-layouts  1.19 us (3%)
  between operations  0.74 us (2%)
    pallas_call x1, Pallas kernels, on_device(): pl.pallas_call(functools.partial(far_kernel, share=share, cells=cells, pa...  9.58 us
    ppermute x4, starting transfers between devices, swapped(): return lax.ppermute(value, 'cells', pairs)  7.19 us
    ppermute x6, starting transfers between devices, from_all(): lax.ppermute(value, 'coef', [(i, i ^ k) for i in range(count)])  6.2 us
    ppermute x6, waiting for transfers between devices, from_all(): lax.ppermute(value, 'coef', [(i, i ^ k) for i in range(count)])  2.83 us
    pallas_call x1, Pallas kernels, on_device(): pl.pallas_call(functools.partial(plan_kernel, cells=cells, noff=noff), ou...  2.75 us
    pallas_call x1, Pallas kernels, on_device(): pl.pallas_call(functools.partial(near_kernel, share=share, cells=cells),...  1.84 us
    ppermute x4, waiting for transfers between devices, swapped(): return lax.ppermute(value, 'cells', pairs)  1.44 us
    add x1, other arithmetic, on_device(): sums = [a + b for a, b in zip(sums[::2], sums[1::2])]  1.3 us
  transfers between devices with their start and end apart: 10, of which 3 were waited for; matrix products, arithmetic and copies ran while one was open for 2% of the time, Pallas kernels for 8%

profile of v3, /device:TPU:13, one launch (start us, length us, event | category | flops | bytes accessed | tf_op | source)
XLA Modules:
  0.0 36.4 jit_solution(7675421999500045908)
XLA Ops:
  0.6 0.0 copy-start.8
  0.6 0.7 %fusion.1.refs_0_ = bf16[48,128]{1,0:T(8,128)(2,1)S(1)} fusion(bf16[16,32]{1,0:T(8,128)(2,1)} %bitcast.8, bf16[32,128]{1,0:T(8,128)(2,1)} %param.7), kind=kLoop, calls=%fused_computation.2 | loop fusion | flops 36864 | bytes 21504 | tf_op jit(solution)/shard_map/concatenate | solution.py:232
  1.4 0.0 copy-start
  1.4 0.7 %collective-permute-start = (bf16[48,128]{1,0:T(8,128)(2,1)S(1)}, bf16[48,128]{1,0:T(8,128)(2,1)S(1)}, u32[]{:S(2)}, u32[]{:S(2)}) collective-permute-start(bf16[48,128]{1,0:T(8,128)(2,1)S(1)} %fusion.1.refs_0_), channel_id=1, source_target_pairs={{0,1},{1,0},{2,3},{3,2},{4,5},{5,4},{6,7},{7,6},{8,9},{9,8},{10,11... | collective-permute-start | bytes 36872 | tf_op jit(solution)/shard_map/ppermute | solution.py:219
  2.0 1.2 %collective-permute-start.1 = (bf16[48,128]{1,0:T(8,128)(2,1)S(1)}, bf16[48,128]{1,0:T(8,128)(2,1)S(1)}, u32[]{:S(2)}, u32[]{:S(2)}) collective-permute-start(bf16[48,128]{1,0:T(8,128)(2,1)S(1)} %fusion.1.refs_0_), channel_id=1, source_target_pairs={{0,2},{1,3},{2,0},{3,1},{4,6},{5,7},{6,4},{7,5},{8,10},{9,11},{10,... | collective-permute-start | bytes 36872 | tf_op jit(solution)/shard_map/ppermute | solution.py:219
  3.3 0.5 %collective-permute-start.2 = (bf16[48,128]{1,0:T(8,128)(2,1)S(1)}, bf16[48,128]{1,0:T(8,128)(2,1)S(1)}, u32[]{:S(2)}, u32[]{:S(2)}) collective-permute-start(bf16[48,128]{1,0:T(8,128)(2,1)S(1)} %fusion.1.refs_0_), channel_id=1, source_target_pairs={{0,3},{1,2},{2,1},{3,0},{4,7},{5,6},{6,5},{7,4},{8,11},{9,10},{10,... | collective-permute-start | bytes 36872 | tf_op jit(solution)/shard_map/ppermute | solution.py:219
  3.7 2.7 %plan.1 = (s32[1,1024]{1,0:T(1,128)}, s32[1,1024]{1,0:T(1,128)}, s32[8,128]{1,0:T(8,128)}) custom-call(s32[189,128]{1,0:T(8,128)} %refs_5_.1), custom_call_target="tpu_custom_call" | custom-call | tf_op jit(solution)/shard_map/plan/pallas_call | solution.py:236
  6.5 0.0 collective-permute-done.refs_1_
  6.5 0.0 copy-start.5
  6.5 0.0 collective-permute-done.1.refs_2_
  6.5 0.0 copy-start.6
  6.5 0.0 collective-permute-done.2.refs_3_
  6.5 0.0 copy-start.7
  6.5 0.0 copy-done
  6.5 0.5 %copy-done.5 = bf16[48,128]{1,0:T(8,128)(2,1)} copy-done((bf16[48,128]{1,0:T(8,128)(2,1)}, bf16[48,128]{1,0:T(8,128)(2,1)S(1)}, u32[]{:S(2)}) %copy-start.5) | copy-done | bytes 12312
  7.1 0.0 copy-done.6
  7.1 0.0 copy-done.7
  7.1 9.6 %far.1 = (f32[32,128]{1,0:T(8,128)}, f32[32,128]{1,0:T(8,128)}, f32[32,128]{1,0:T(8,128)}, f32[32,128]{1,0:T(8,128)}, f32[32,128]{1,0:T(8,128)}) custom-call(bf16[48,128]{1,0:T(8,128)(2,1)} %copy-done, bf16[48,128]{1,0:T(8,128)(2,1)} %copy-done.5, bf16[48,128]{1,0:T(8,128)(2,1)} %copy-done.6, bf16[48,128]{1,0:T(8,128)(2,1)} %copy-done.7, ...), custom_call_target="tpu_custom_call" | custom-call | tf_op jit(solution)/shard_map/far/pallas_call | solution.py:249
  16.7 0.3 collective-permute-start.3
  17.0 3.8 %collective-permute-start.4 = (f32[32,128]{1,0:T(8,128)}, f32[32,128]{1,0:T(8,128)S(1)}, u32[]{:S(2)}, u32[]{:S(2)}) collective-permute-start(f32[32,128]{1,0:T(8,128)} %get-tuple-element.17), channel_id=1, source_target_pairs={{4,8},{8,4},{12,16},{16,12},{20,24},{24,20},{5,9},{9,5},{13,17},{1... | collective-permute-start | bytes 49160 | tf_op jit(solution)/shard_map/ppermute | solution.py:213
  20.8 0.5 %collective-permute-start.5 = (f32[32,128]{1,0:T(8,128)}, f32[32,128]{1,0:T(8,128)S(1)}, u32[]{:S(2)}, u32[]{:S(2)}) collective-permute-start(f32[32,128]{1,0:T(8,128)} %get-tuple-element.18), channel_id=1, source_target_pairs={{0,8},{8,0},{4,12},{12,4},{16,24},{24,16},{20,28},{28,20},{1,9},{9... | collective-permute-start | bytes 49160 | tf_op jit(solution)/shard_map/ppermute | solution.py:213
  21.3 2.6 %collective-permute-start.6 = (f32[32,128]{1,0:T(8,128)}, f32[32,128]{1,0:T(8,128)S(1)}, u32[]{:S(2)}, u32[]{:S(2)}) collective-permute-start(f32[32,128]{1,0:T(8,128)} %get-tuple-element.19), channel_id=1, source_target_pairs={{8,16},{16,8},{12,20},{20,12},{9,17},{17,9},{13,21},{21,13},{10,18... | collective-permute-start | bytes 49160 | tf_op jit(solution)/shard_map/ppermute | solution.py:213
  23.9 0.0 copy-done.8
  23.9 0.6 %broadcast_subtract_fusion = s32[2048]{0:T(1024)} fusion(s32[2048]{0:T(1024)S(1)} %copy-done.8, s32[]{:T(128)S(6)} %mul.3), kind=kLoop, calls=%fused_computation.4 | loop fusion | flops 2048 | bytes 16388 | tf_op jit(solution)/shard_map/sub | solution.py:273
  24.5 0.0 collective-permute-done.3.refs_1_
  24.5 0.0 copy-start.1
  24.5 0.0 collective-permute-done.4.refs_2_
  24.5 0.0 copy-start.2
  24.5 0.0 collective-permute-done.5.refs_3_
  24.6 0.0 copy-start.3
  24.6 1.4 %collective-permute-done.6.refs_4_ = f32[32,128]{1,0:T(8,128)S(1)} collective-permute-done((f32[32,128]{1,0:T(8,128)}, f32[32,128]{1,0:T(8,128)S(1)}, u32[]{:S(2)}, u32[]{:S(2)}) %collective-permute-start.6) | collective-permute-done | bytes 16416 | tf_op jit(solution)/shard_map/ppermute | solution.py:213
  26.0 0.0 copy-start.4
  26.0 0.0 copy-done.1
  26.0 0.0 copy-done.2
  26.0 0.0 copy-done.3
  26.0 0.6 %copy-done.4 = f32[32,128]{1,0:T(8,128)} copy-done((f32[32,128]{1,0:T(8,128)}, f32[32,128]{1,0:T(8,128)S(1)}, u32[]{:S(2)}) %copy-start.4) | copy-done | bytes 16408
  26.6 1.8 %near.1 = (f32[32,128]{1,0:T(8,128)}, f32[1,2048]{1,0:T(1,128)}) custom-call(f32[32,128]{1,0:T(8,128)} %get-tuple-element.15.refs_0_, f32[32,128]{1,0:T(8,128)} %copy-done.1, f32[32,128]{1,0:T(8,128)} %copy-done.2, f32[32,128]{1,0:T(8,128)} %copy-done.3, f32[32,128]{1,0:T(8,128)} %copy-done.4, s32[1,2048]{1,0:T(1,128)} %bitcast.3, bf16[32,2048]{1,0:T(8,128)(2,1)} %refs_6_.3), custom_call_target="tpu_custom_call" | custom-call | tf_op jit(solution)/shard_map/near/pallas_call | solution.py:275
  28.4 2.2 %collective-permute-start.7 = (f32[2048]{0:T(1024)}, f32[2048]{0:T(1024)S(1)}, u32[]{:S(2)}, u32[]{:S(2)}) collective-permute-start(f32[2048]{0:T(1024)} %bitcast.4), channel_id=1, source_target_pairs={{0,1},{1,0},{2,3},{3,2},{4,5},{5,4},{6,7},{7,6},{8,9},{9,8},{10,11... | collective-permute-start | bytes 24584 | tf_op jit(solution)/shard_map/ppermute | solution.py:219
  30.6 1.2 %collective-permute-start.8 = (f32[2048]{0:T(1024)}, f32[2048]{0:T(1024)S(1)}, u32[]{:S(2)}, u32[]{:S(2)}) collective-permute-start(f32[2048]{0:T(1024)} %bitcast.5), channel_id=1, source_target_pairs={{0,2},{1,3},{2,0},{3,1},{4,6},{5,7},{6,4},{7,5},{8,10},{9,11},{10,... | collective-permute-start | bytes 24584 | tf_op jit(solution)/shard_map/ppermute | solution.py:219
  31.8 0.5 %collective-permute-start.9 = (f32[2048]{0:T(1024)}, f32[2048]{0:T(1024)S(1)}, u32[]{:S(2)}, u32[]{:S(2)}) collective-permute-start(f32[2048]{0:T(1024)} %bitcast.6), channel_id=1, source_target_pairs={{0,3},{1,2},{2,1},{3,0},{4,7},{5,6},{6,5},{7,4},{8,11},{9,10},{10,... | collective-permute-start | bytes 24584 | tf_op jit(solution)/shard_map/ppermute | solution.py:219
  32.3 0.0 collective-permute-done.7
  32.3 1.1 %collective-permute-done.8 = f32[2048]{0:T(1024)S(1)} collective-permute-done((f32[2048]{0:T(1024)}, f32[2048]{0:T(1024)S(1)}, u32[]{:S(2)}, u32[]{:S(2)}) %collective-permute-start.8) | collective-permute-done | bytes 8224 | tf_op jit(solution)/shard_map/ppermute | solution.py:219
  33.3 1.7 %collective-permute-done.9 = f32[2048]{0:T(1024)S(1)} collective-permute-done((f32[2048]{0:T(1024)}, f32[2048]{0:T(1024)S(1)}, u32[]{:S(2)}, u32[]{:S(2)}) %collective-permute-start.9) | collective-permute-done | bytes 8224 | tf_op jit(solution)/shard_map/ppermute | solution.py:219
  35.1 1.3 %add_add_fusion = f32[2048]{0:T(1024)} fusion(f32[2048]{0:T(1024)S(1)} %collective-permute-done.8, f32[2048]{0:T(1024)S(1)} %collective-permute-done.9, f32[2048]{0:T(1024)} %bitcast.7, f32[2048]{0:T(1024)S(1)} %collective-permute-done.7), kind=kLoop, calls=%fused_computation.3 | loop fusion | flops 6144 | bytes 40960 | tf_op jit(solution)/shard_map/add | solution.py:287
Async XLA Ops:
  0.6 23.3 %copy-start.8 = (s32[2048]{0:T(1024)S(1)}, s32[2048]{0:T(1024)}, u32[]{:S(2)}) copy-start(s32[2048]{0:T(1024)} %param.12) | copy-start | bytes 24580
  1.4 5.2 %copy-start = (bf16[48,128]{1,0:T(8,128)(2,1)}, bf16[48,128]{1,0:T(8,128)(2,1)S(1)}, u32[]{:S(2)}) copy-start(bf16[48,128]{1,0:T(8,128)(2,1)S(1)} %fusion.1.refs_0_) | copy-start | bytes 36868
  1.4 5.1 %collective-permute-start = (bf16[48,128]{1,0:T(8,128)(2,1)S(1)}, bf16[48,128]{1,0:T(8,128)(2,1)S(1)}, u32[]{:S(2)}, u32[]{:S(2)}) collective-permute-start(bf16[48,128]{1,0:T(8,128)(2,1)S(1)} %fusion.1.refs_0_), channel_id=1, source_target_pairs={{0,1},{1,0},{2,3},{3,2},{4,5},{5,4},{6,7},{7,6},{8,9},{9,8},{10,11... | collective-permute-start | bytes 36872 | tf_op jit(solution)/shard_map/ppermute | solution.py:219
  2.0 4.5 %collective-permute-start.1 = (bf16[48,128]{1,0:T(8,128)(2,1)S(1)}, bf16[48,128]{1,0:T(8,128)(2,1)S(1)}, u32[]{:S(2)}, u32[]{:S(2)}) collective-permute-start(bf16[48,128]{1,0:T(8,128)(2,1)S(1)} %fusion.1.refs_0_), channel_id=1, source_target_pairs={{0,2},{1,3},{2,0},{3,1},{4,6},{5,7},{6,4},{7,5},{8,10},{9,11},{10,... | collective-permute-start | bytes 36872 | tf_op jit(solution)/shard_map/ppermute | solution.py:219
  3.3 3.3 %collective-permute-start.2 = (bf16[48,128]{1,0:T(8,128)(2,1)S(1)}, bf16[48,128]{1,0:T(8,128)(2,1)S(1)}, u32[]{:S(2)}, u32[]{:S(2)}) collective-permute-start(bf16[48,128]{1,0:T(8,128)(2,1)S(1)} %fusion.1.refs_0_), channel_id=1, source_target_pairs={{0,3},{1,2},{2,1},{3,0},{4,7},{5,6},{6,5},{7,4},{8,11},{9,10},{10,... | collective-permute-start | bytes 36872 | tf_op jit(solution)/shard_map/ppermute | solution.py:219
  6.5 0.6 %copy-start.5 = (bf16[48,128]{1,0:T(8,128)(2,1)}, bf16[48,128]{1,0:T(8,128)(2,1)S(1)}, u32[]{:S(2)}) copy-start(bf16[48,128]{1,0:T(8,128)(2,1)S(1)} %collective-permute-done.refs_1_) | copy-start | bytes 36868
  6.5 0.6 %copy-start.6 = (bf16[48,128]{1,0:T(8,128)(2,1)}, bf16[48,128]{1,0:T(8,128)(2,1)S(1)}, u32[]{:S(2)}) copy-start(bf16[48,128]{1,0:T(8,128)(2,1)S(1)} %collective-permute-done.1.refs_2_) | copy-start | bytes 36868
  6.5 0.6 %copy-start.7 = (bf16[48,128]{1,0:T(8,128)(2,1)}, bf16[48,128]{1,0:T(8,128)(2,1)S(1)}, u32[]{:S(2)}) copy-start(bf16[48,128]{1,0:T(8,128)(2,1)S(1)} %collective-permute-done.2.refs_3_) | copy-start | bytes 36868
  16.7 7.8 %collective-permute-start.3 = (f32[32,128]{1,0:T(8,128)}, f32[32,128]{1,0:T(8,128)S(1)}, u32[]{:S(2)}, u32[]{:S(2)}) collective-permute-start(f32[32,128]{1,0:T(8,128)} %get-tuple-element.16), channel_id=1, source_target_pairs={{0,4},{4,0},{8,12},{12,8},{16,20},{20,16},{24,28},{28,24},{1,5},{5... | collective-permute-start | bytes 49160 | tf_op jit(solution)/shard_map/ppermute | solution.py:213
  17.0 7.6 %collective-permute-start.4 = (f32[32,128]{1,0:T(8,128)}, f32[32,128]{1,0:T(8,128)S(1)}, u32[]{:S(2)}, u32[]{:S(2)}) collective-permute-start(f32[32,128]{1,0:T(8,128)} %get-tuple-element.17), channel_id=1, source_target_pairs={{4,8},{8,4},{12,16},{16,12},{20,24},{24,20},{5,9},{9,5},{13,17},{1... | collective-permute-start | bytes 49160 | tf_op jit(solution)/shard_map/ppermute | solution.py:213
  20.8 3.7 %collective-permute-start.5 = (f32[32,128]{1,0:T(8,128)}, f32[32,128]{1,0:T(8,128)S(1)}, u32[]{:S(2)}, u32[]{:S(2)}) collective-permute-start(f32[32,128]{1,0:T(8,128)} %get-tuple-element.18), channel_id=1, source_target_pairs={{0,8},{8,0},{4,12},{12,4},{16,24},{24,16},{20,28},{28,20},{1,9},{9... | collective-permute-start | bytes 49160 | tf_op jit(solution)/shard_map/ppermute | solution.py:213
  21.3 4.7 %collective-permute-start.6 = (f32[32,128]{1,0:T(8,128)}, f32[32,128]{1,0:T(8,128)S(1)}, u32[]{:S(2)}, u32[]{:S(2)}) collective-permute-start(f32[32,128]{1,0:T(8,128)} %get-tuple-element.19), channel_id=1, source_target_pairs={{8,16},{16,8},{12,20},{20,12},{9,17},{17,9},{13,21},{21,13},{10,18... | collective-permute-start | bytes 49160 | tf_op jit(solution)/shard_map/ppermute | solution.py:213
  24.5 1.5 %copy-start.1 = (f32[32,128]{1,0:T(8,128)}, f32[32,128]{1,0:T(8,128)S(1)}, u32[]{:S(2)}) copy-start(f32[32,128]{1,0:T(8,128)S(1)} %collective-permute-done.3.refs_1_) | copy-start | bytes 49156
  24.5 1.5 %copy-start.2 = (f32[32,128]{1,0:T(8,128)}, f32[32,128]{1,0:T(8,128)S(1)}, u32[]{:S(2)}) copy-start(f32[32,128]{1,0:T(8,128)S(1)} %collective-permute-done.4.refs_2_) | copy-start | bytes 49156
  24.6 1.5 %copy-start.3 = (f32[32,128]{1,0:T(8,128)}, f32[32,128]{1,0:T(8,128)S(1)}, u32[]{:S(2)}) copy-start(f32[32,128]{1,0:T(8,128)S(1)} %collective-permute-done.5.refs_3_) | copy-start | bytes 49156
  26.0 0.6 %copy-start.4 = (f32[32,128]{1,0:T(8,128)}, f32[32,128]{1,0:T(8,128)S(1)}, u32[]{:S(2)}) copy-start(f32[32,128]{1,0:T(8,128)S(1)} %collective-permute-done.6.refs_4_) | copy-start | bytes 49156
  28.4 3.8 %collective-permute-start.7 = (f32[2048]{0:T(1024)}, f32[2048]{0:T(1024)S(1)}, u32[]{:S(2)}, u32[]{:S(2)}) collective-permute-start(f32[2048]{0:T(1024)} %bitcast.4), channel_id=1, source_target_pairs={{0,1},{1,0},{2,3},{3,2},{4,5},{5,4},{6,7},{7,6},{8,9},{9,8},{10,11... | collective-permute-start | bytes 24584 | tf_op jit(solution)/shard_map/ppermute | solution.py:219
  30.6 2.7 %collective-permute-start.8 = (f32[2048]{0:T(1024)}, f32[2048]{0:T(1024)S(1)}, u32[]{:S(2)}, u32[]{:S(2)}) collective-permute-start(f32[2048]{0:T(1024)} %bitcast.5), channel_id=1, source_target_pairs={{0,2},{1,3},{2,0},{3,1},{4,6},{5,7},{6,4},{7,5},{8,10},{9,11},{10,... | collective-permute-start | bytes 24584 | tf_op jit(solution)/shard_map/ppermute | solution.py:219
  31.8 3.3 %collective-permute-start.9 = (f32[2048]{0:T(1024)}, f32[2048]{0:T(1024)S(1)}, u32[]{:S(2)}, u32[]{:S(2)}) collective-permute-start(f32[2048]{0:T(1024)} %bitcast.6), channel_id=1, source_target_pairs={{0,3},{1,2},{2,1},{3,0},{4,7},{5,6},{6,5},{7,4},{8,11},{9,10},{10,... | collective-permute-start | bytes 24584 | tf_op jit(solution)/shard_map/ppermute | solution.py:219

commit v4 on v3

--- a/solution.py
+++ b/solution.py
@@ -20,6 +20,14 @@
         side = (index // length) % 2
         steps += [length * (1 - 2 * side), length * (2 * side - 1)]
     return steps
+
+
+def started(sources, targets, sems):
+    copies = []
+    for i, (source, target) in enumerate(zip(sources, targets)):
+        copies.append(pltpu.make_async_copy(source, target, sems.at[i]))
+        copies[-1].start()
+    return copies
 
 
 def ones_where(mask):
@@ -74,10 +82,13 @@
 
 def far_kernel(*refs, share, cells, parents, noff, coefs):
     f32, bf16, i32 = jnp.float32, jnp.bfloat16, jnp.int32
-    shards = refs[:coefs]
-    ops_ref, tgt_ref, l2l_ref, row_ref, code_ref, total_ref = refs[coefs : coefs + 6]
+    row_ref, total_ref = refs[coefs + 4 : coefs + 6]
     outs = refs[coefs + 6 : coefs + 6 + BLOCKS]
-    poles, spread_parents, poles_t, hot, rhs, acc, terms, picked, far = refs[coefs + 6 + BLOCKS :]
+    scratch = refs[coefs + 6 + BLOCKS :]
+    sems, shard_buf, ops_ref, tgt_ref, l2l_ref, code_ref = scratch[:6]
+    poles, spread_parents, poles_t, hot, rhs, acc, terms, picked, far = scratch[6:]
+    targets = [shard_buf.at[k] for k in range(coefs)] + [ops_ref, tgt_ref, l2l_ref, code_ref]
+    copies = started(refs[: coefs + 4], targets, sems)
     cell_index = lax.axis_index("cells")
     coef_index = lax.axis_index("coef")
     lanes = 4 * share
@@ -85,16 +96,20 @@
     src = lax.broadcasted_iota(i32, (parents, cells), 0)
     dst = lax.broadcasted_iota(i32, (parents, cells), 1)
     spread = ones_where(dst // children == src)
+    acc[...] = jnp.zeros_like(acc)
+    picked[...] = jnp.zeros_like(picked)
+    for k in range(coefs):
+        copies[k].wait()
     for k in range(coefs):
         at = pl.multiple_of((coef_index ^ k) * share, share)
-        shard = shards[k][...]
+        shard = shard_buf[k]
         poles[pl.ds(at, share), :] = shard[:share, :]
         spread_parents[pl.ds(at, share), :] = lax.dot_general(
             shard[share:, :], spread, (((0,), (0,)), ((), ())), preferred_element_type=f32
         )[:share]
     poles_t[...] = poles[...].astype(f32).T.astype(bf16)
-    acc[...] = jnp.zeros_like(acc)
-    picked[...] = jnp.zeros_like(picked)
+    for copy in copies[coefs:]:
+        copy.wait()
     rows = lax.broadcasted_iota(i32, (cells, cells), 0).astype(f32).astype(bf16)
     lane = lax.broadcasted_iota(i32, (cells, lanes), 1)
     is_high = (lane % (2 * share)) < share
@@ -186,20 +201,24 @@
 
 
 def near_kernel(*refs, share, cells):
-    pieces = refs[:BLOCKS]
-    leaf_ref, basis_ref, out_ref, pot_ref = refs[BLOCKS:]
+    out_ref, pot_ref, sems, pieces, leaf_ref, basis_ref, hot = refs[BLOCKS + 2 :]
     f32, bf16 = jnp.float32, jnp.bfloat16
-    leaf = pieces[0][...]
-    for piece in pieces[1:]:
-        leaf = leaf + piece[...]
+    targets = [leaf_ref, basis_ref] + [pieces.at[k] for k in range(BLOCKS)]
+    copies = started(refs[: BLOCKS + 2], targets, sems)
+    copies[0].wait()
+    count = leaf_ref.shape[1]
+    rows = lax.broadcasted_iota(jnp.int32, (cells, count), 0)
+    hot[...] = ones_where(rows == leaf_ref[...] - lax.axis_index("cells") * cells)
+    for copy in copies[1:]:
+        copy.wait()
+    leaf = pieces[0]
+    for k in range(1, BLOCKS):
+        leaf = leaf + pieces[k]
     out_ref[...] = leaf
     high = leaf.astype(bf16)
     low = (leaf - high.astype(f32)).astype(bf16)
     both = jnp.concatenate([high, low], axis=0)
-    count = leaf_ref.shape[1]
-    rows = lax.broadcasted_iota(jnp.int32, (cells, count), 0)
-    hot = jnp.where(rows == leaf_ref[...], 1.0, 0.0).astype(bf16)
-    columns = jnp.dot(both, hot, preferred_element_type=f32)
+    columns = jnp.dot(both, hot[...], preferred_element_type=f32)
     columns = columns[:share] + columns[share:]
     pot_ref[...] = jnp.sum(columns * basis_ref[...].astype(f32), axis=0, keepdims=True)
 
@@ -207,9 +226,10 @@
 def swapped(value, length, phase):
     count = lax.axis_size("cells")
     pairs = []
-    for low in range(count - length):
+    for low in range(count):
         if (low // length) % 2 == phase:
-            pairs += [(low, low + length), (low + length, low)]
+            high = (low + length) % count
+            pairs += [(low, high), (high, low)]
     return lax.ppermute(value, "cells", pairs)
 
 
@@ -223,7 +243,6 @@
 def on_device(
     multipole, parent_local, m2l_ops, l2l_ops, target_cell, particle_leaf, particle_basis
 ):
-    my_index = lax.axis_index("cells")
     cells = multipole.shape[1]
     parents = parent_local.shape[1]
     coefs = lax.axis_size("coef")
@@ -231,6 +250,7 @@
     flipped = jnp.pad(parent_local.T, ((0, 0), (0, cells - share)))
     shards = from_all(jnp.concatenate([multipole, flipped], axis=0))
     vmem = pl.BlockSpec(memory_space=pltpu.VMEM)
+    anywhere = pl.BlockSpec(memory_space=pl.ANY)
     smem = pl.BlockSpec(memory_space=pltpu.SMEM)
     i32 = jnp.int32
     rows, codes, total = pl.pallas_call(
@@ -251,9 +271,15 @@
             far_kernel, share=share, cells=cells, parents=parents, noff=noff, coefs=coefs
         ),
         out_shape=[jax.ShapeDtypeStruct((share, cells), jnp.float32)] * BLOCKS,
-        in_specs=[vmem] * (coefs + 3) + [smem, vmem, smem],
+        in_specs=[anywhere] * (coefs + 4) + [smem, smem],
         out_specs=[vmem] * BLOCKS,
         scratch_shapes=[
+            pltpu.SemaphoreType.DMA((coefs + 4,)),
+            pltpu.VMEM((coefs,) + shards[0].shape, jnp.bfloat16),
+            pltpu.VMEM(m2l_ops.shape, jnp.bfloat16),
+            pltpu.VMEM(target_cell.shape, i32),
+            pltpu.VMEM(l2l_ops.shape, jnp.bfloat16),
+            pltpu.VMEM((1, SLOTS), i32),
             pltpu.VMEM((width, cells), jnp.bfloat16),
             pltpu.VMEM((width, cells), jnp.float32),
             pltpu.VMEM((cells, width), jnp.bfloat16),
@@ -265,12 +291,12 @@
             pltpu.VMEM((2 * REACH * cells, lanes), jnp.float32),
         ],
         name="far",
-    )(*shards, m2l_ops, target_cell, l2l_ops, rows, codes, total)
+    )(*shards, m2l_ops, target_cell, l2l_ops, codes, rows, total)
     pieces = [blocks[0]]
     for length in range(1, REACH + 1):
         for phase in range(2):
             pieces.append(swapped(blocks[2 * length - 1 + phase], length, phase))
-    index = (particle_leaf - my_index * cells).reshape(1, -1)
+    index = particle_leaf.reshape(1, -1)
     count = index.shape[1]
     leaf_local, partial = pl.pallas_call(
         functools.partial(near_kernel, share=share, cells=cells),
@@ -278,10 +304,17 @@
             jax.ShapeDtypeStruct((share, cells), jnp.float32),
             jax.ShapeDtypeStruct((1, count), jnp.float32),
         ],
-        in_specs=[vmem] * (BLOCKS + 2),
+        in_specs=[anywhere] * (BLOCKS + 2),
         out_specs=[vmem] * 2,
+        scratch_shapes=[
+            pltpu.SemaphoreType.DMA((BLOCKS + 2,)),
+            pltpu.VMEM((BLOCKS, share, cells), jnp.float32),
+            pltpu.VMEM((1, count), i32),
+            pltpu.VMEM((share, count), jnp.bfloat16),
+            pltpu.VMEM((cells, count), jnp.bfloat16),
+        ],
         name="near",
-    )(*pieces, index, particle_basis)
+    )(index, particle_basis, *pieces)
     sums = from_all(partial.reshape(-1))
     while len(sums) > 1:
         sums = [a + b for a, b in zip(sums[::2], sums[1::2])]

time: 36.7 us -> 37.2 us (1.014)
  the two profiles are of different devices: /device:TPU:13 before, /device:TPU:0 now
where the time goes in v4:
time: 37.2 us; the launch traced here: 36.8 us
  Pallas kernels  14.4 us (39%)
  starting transfers between devices  11.3 us (30%)
  waiting for transfers between devices  7.17 us (19%)
  other arithmetic  2.02 us (5%)
  local copies, waits for them, and re-layouts  1.21 us (3%)
  between operations  0.68 us (2%)
    pallas_call x1, Pallas kernels, on_device(): pl.pallas_call(functools.partial(far_kernel, share=share, cells=cells, pa...  9.8 us
    ppermute x4, starting transfers between devices, swapped(): return lax.ppermute(value, 'cells', pairs)  6.32 us
    ppermute x6, starting transfers between devices, from_all(): lax.ppermute(value, 'coef', [(i, i ^ k) for i in range(count)])  5 us
    ppermute x4, waiting for transfers between devices, swapped(): return lax.ppermute(value, 'cells', pairs)  4.83 us
    pallas_call x1, Pallas kernels, on_device(): pl.pallas_call(functools.partial(plan_kernel, cells=cells, noff=noff), ou...  2.76 us
    ppermute x6, waiting for transfers between devices, from_all(): lax.ppermute(value, 'coef', [(i, i ^ k) for i in range(count)])  2.34 us
    pallas_call x1, Pallas kernels, on_device(): pl.pallas_call(functools.partial(near_kernel, share=share, cells=cells),...  1.83 us
    add x1, other arithmetic, on_device(): sums = [a + b for a, b in zip(sums[::2], sums[1::2])]  1.3 us
  transfers between devices with their start and end apart: 10, of which 6 were waited for; matrix products, arithmetic and copies ran while one was open for 0% of the time, Pallas kernels for 7%

profile of v4, /device:TPU:0, one launch (start us, length us, event | category | flops | bytes accessed | tf_op | source)
XLA Modules:
  0.0 36.8 jit_solution(8571016663259212107)
XLA Ops:
  0.6 0.7 %fusion.1.refs_0_ = bf16[48,128]{1,0:T(8,128)(2,1)S(1)} fusion(bf16[16,32]{1,0:T(8,128)(2,1)} %bitcast.8, bf16[32,128]{1,0:T(8,128)(2,1)} %param.7), kind=kLoop, calls=%fused_computation.2 | loop fusion | flops 36864 | bytes 21504 | tf_op jit(solution)/shard_map/concatenate | solution.py:251
  1.4 0.0 copy-start
  1.4 2.4 %collective-permute-start.2 = (bf16[48,128]{1,0:T(8,128)(2,1)S(1)}, bf16[48,128]{1,0:T(8,128)(2,1)S(1)}, u32[]{:S(2)}, u32[]{:S(2)}) collective-permute-start(bf16[48,128]{1,0:T(8,128)(2,1)S(1)} %fusion.1.refs_0_), channel_id=1, source_target_pairs={{0,3},{1,2},{2,1},{3,0},{4,7},{5,6},{6,5},{7,4},{8,11},{9,10},{10,... | collective-permute-start | bytes 36872 | tf_op jit(solution)/shard_map/ppermute | solution.py:239
  3.8 0.6 %collective-permute-start.1 = (bf16[48,128]{1,0:T(8,128)(2,1)S(1)}, bf16[48,128]{1,0:T(8,128)(2,1)S(1)}, u32[]{:S(2)}, u32[]{:S(2)}) collective-permute-start(bf16[48,128]{1,0:T(8,128)(2,1)S(1)} %fusion.1.refs_0_), channel_id=1, source_target_pairs={{0,2},{1,3},{2,0},{3,1},{4,6},{5,7},{6,4},{7,5},{8,10},{9,11},{10,... | collective-permute-start | bytes 36872 | tf_op jit(solution)/shard_map/ppermute | solution.py:239
  4.4 0.0 collective-permute-start
  4.4 2.8 %plan.1 = (s32[1,1024]{1,0:T(1,128)}, s32[1,1024]{1,0:T(1,128)}, s32[8,128]{1,0:T(8,128)}) custom-call(s32[189,128]{1,0:T(8,128)} %refs_5_.1), custom_call_target="tpu_custom_call" | custom-call | tf_op jit(solution)/shard_map/plan/pallas_call | solution.py:256
  7.2 0.0 collective-permute-done.2.refs_3_
  7.2 0.0 copy-start.5
  7.2 0.3 collective-permute-done.1.refs_2_
  7.5 0.0 copy-start.6
  7.5 0.0 collective-permute-done.refs_1_
  7.5 0.0 copy-start.7
  7.5 0.0 copy-done
  7.5 0.3 copy-done.5
  7.8 0.3 copy-done.6
  8.1 0.0 copy-done.7
  8.1 9.8 %far.1 = (f32[32,128]{1,0:T(8,128)}, f32[32,128]{1,0:T(8,128)}, f32[32,128]{1,0:T(8,128)}, f32[32,128]{1,0:T(8,128)}, f32[32,128]{1,0:T(8,128)}) custom-call(bf16[48,128]{1,0:T(8,128)(2,1)} %copy-done, bf16[48,128]{1,0:T(8,128)(2,1)} %copy-done.7, bf16[48,128]{1,0:T(8,128)(2,1)} %copy-done.6, bf16[48,128]{1,0:T(8,128)(2,1)} %copy-done.5, ...), custom_call_target="tpu_custom_call" | custom-call | tf_op jit(solution)/shard_map/far/pallas_call | solution.py:269
  17.9 1.9 %collective-permute-start.3 = (f32[32,128]{1,0:T(8,128)}, f32[32,128]{1,0:T(8,128)S(1)}, u32[]{:S(2)}, u32[]{:S(2)}) collective-permute-start(f32[32,128]{1,0:T(8,128)} %get-tuple-element.16), channel_id=1, source_target_pairs={{0,4},{4,0},{8,12},{12,8},{16,20},{20,16},{24,28},{28,24},{1,5},{5... | collective-permute-start | bytes 49160 | tf_op jit(solution)/shard_map/ppermute | solution.py:233
  19.7 3.6 %collective-permute-start.4 = (f32[32,128]{1,0:T(8,128)}, f32[32,128]{1,0:T(8,128)S(1)}, u32[]{:S(2)}, u32[]{:S(2)}) collective-permute-start(f32[32,128]{1,0:T(8,128)} %get-tuple-element.17), channel_id=1, source_target_pairs={{4,8},{8,4},{12,16},{16,12},{20,24},{24,20},{28,0},{0,28},{5,9},{9... | collective-permute-start | bytes 49160 | tf_op jit(solution)/shard_map/ppermute | solution.py:233
  23.3 0.0 collective-permute-start.5
  23.3 0.9 %collective-permute-start.6 = (f32[32,128]{1,0:T(8,128)}, f32[32,128]{1,0:T(8,128)S(1)}, u32[]{:S(2)}, u32[]{:S(2)}) collective-permute-start(f32[32,128]{1,0:T(8,128)} %get-tuple-element.19), channel_id=1, source_target_pairs={{8,16},{16,8},{12,20},{20,12},{24,0},{0,24},{28,4},{4,28},{9,17},{... | collective-permute-start | bytes 49160 | tf_op jit(solution)/shard_map/ppermute | solution.py:233
  24.2 0.0 collective-permute-done.3.refs_3_
  24.2 0.0 copy-start.1
  24.2 2.2 %collective-permute-done.4.refs_4_ = f32[32,128]{1,0:T(8,128)S(1)} collective-permute-done((f32[32,128]{1,0:T(8,128)}, f32[32,128]{1,0:T(8,128)S(1)}, u32[]{:S(2)}, u32[]{:S(2)}) %collective-permute-start.4) | collective-permute-done | bytes 16416 | tf_op jit(solution)/shard_map/ppermute | solution.py:233
  26.4 0.0 copy-start.2
  26.4 0.8 %collective-permute-done.5.refs_5_ = f32[32,128]{1,0:T(8,128)S(1)} collective-permute-done((f32[32,128]{1,0:T(8,128)}, f32[32,128]{1,0:T(8,128)S(1)}, u32[]{:S(2)}, u32[]{:S(2)}) %collective-permute-start.5) | collective-permute-done | bytes 16416 | tf_op jit(solution)/shard_map/ppermute | solution.py:233
  27.2 0.0 copy-start.3
  27.2 1.8 %collective-permute-done.6.refs_6_ = f32[32,128]{1,0:T(8,128)S(1)} collective-permute-done((f32[32,128]{1,0:T(8,128)}, f32[32,128]{1,0:T(8,128)S(1)}, u32[]{:S(2)}, u32[]{:S(2)}) %collective-permute-start.6) | collective-permute-done | bytes 16416 | tf_op jit(solution)/shard_map/ppermute | solution.py:233
  29.0 0.0 copy-start.4
  29.0 0.0 copy-done.1
  29.0 0.0 copy-done.2
  29.0 0.0 copy-done.3
  29.0 0.6 %copy-done.4 = f32[32,128]{1,0:T(8,128)} copy-done((f32[32,128]{1,0:T(8,128)}, f32[32,128]{1,0:T(8,128)S(1)}, u32[]{:S(2)}) %copy-start.4) | copy-done | bytes 16408
  29.6 1.8 %near.1 = (f32[32,128]{1,0:T(8,128)}, f32[1,2048]{1,0:T(1,128)}) custom-call(s32[1,2048]{1,0:T(1,128)} %bitcast.3, bf16[32,2048]{1,0:T(8,128)(2,1)} %refs_1_.1, f32[32,128]{1,0:T(8,128)} %get-tuple-element.15.refs_2_, f32[32,128]{1,0:T(8,128)} %copy-done.1, f32[32,128]{1,0:T(8,128)} %copy-done.2, f32[32,128]{1,0:T(8,128)} %copy-done.3, f32[32,128]{1,0:T(8,128)} %copy-done.4), custom_call_target="tpu_custom_call" | custom-call | tf_op jit(solution)/shard_map/near/pallas_call | solution.py:301
  31.5 0.1 collective-permute-start.9
  31.5 1.6 %collective-permute-start.8 = (f32[2048]{0:T(1024)}, f32[2048]{0:T(1024)S(1)}, u32[]{:S(2)}, u32[]{:S(2)}) collective-permute-start(f32[2048]{0:T(1024)} %bitcast.5), channel_id=1, source_target_pairs={{0,2},{1,3},{2,0},{3,1},{4,6},{5,7},{6,4},{7,5},{8,10},{9,11},{10,... | collective-permute-start | bytes 24584 | tf_op jit(solution)/shard_map/ppermute | solution.py:239
  33.1 0.3 collective-permute-start.7
  33.4 1.5 %collective-permute-done.9 = f32[2048]{0:T(1024)S(1)} collective-permute-done((f32[2048]{0:T(1024)}, f32[2048]{0:T(1024)S(1)}, u32[]{:S(2)}, u32[]{:S(2)}) %collective-permute-start.9) | collective-permute-done | bytes 8224 | tf_op jit(solution)/shard_map/ppermute | solution.py:239
  34.9 0.6 %collective-permute-done.8 = f32[2048]{0:T(1024)S(1)} collective-permute-done((f32[2048]{0:T(1024)}, f32[2048]{0:T(1024)S(1)}, u32[]{:S(2)}, u32[]{:S(2)}) %collective-permute-start.8) | collective-permute-done | bytes 8224 | tf_op jit(solution)/shard_map/ppermute | solution.py:239
  35.5 0.0 collective-permute-done.7
  35.5 1.3 %add_add_fusion = f32[2048]{0:T(1024)} fusion(f32[2048]{0:T(1024)S(1)} %collective-permute-done.8, f32[2048]{0:T(1024)S(1)} %collective-permute-done.9, f32[2048]{0:T(1024)} %bitcast.7, f32[2048]{0:T(1024)S(1)} %collective-permute-done.7), kind=kLoop, calls=%fused_computation.3 | loop fusion | flops 6144 | bytes 40960 | tf_op jit(solution)/shard_map/add | solution.py:320
Async XLA Ops:
  1.4 6.1 %copy-start = (bf16[48,128]{1,0:T(8,128)(2,1)}, bf16[48,128]{1,0:T(8,128)(2,1)S(1)}, u32[]{:S(2)}) copy-start(bf16[48,128]{1,0:T(8,128)(2,1)S(1)} %fusion.1.refs_0_) | copy-start | bytes 36868
  1.4 5.8 %collective-permute-start.2 = (bf16[48,128]{1,0:T(8,128)(2,1)S(1)}, bf16[48,128]{1,0:T(8,128)(2,1)S(1)}, u32[]{:S(2)}, u32[]{:S(2)}) collective-permute-start(bf16[48,128]{1,0:T(8,128)(2,1)S(1)} %fusion.1.refs_0_), channel_id=1, source_target_pairs={{0,3},{1,2},{2,1},{3,0},{4,7},{5,6},{6,5},{7,4},{8,11},{9,10},{10,... | collective-permute-start | bytes 36872 | tf_op jit(solution)/shard_map/ppermute | solution.py:239
  3.8 3.7 %collective-permute-start.1 = (bf16[48,128]{1,0:T(8,128)(2,1)S(1)}, bf16[48,128]{1,0:T(8,128)(2,1)S(1)}, u32[]{:S(2)}, u32[]{:S(2)}) collective-permute-start(bf16[48,128]{1,0:T(8,128)(2,1)S(1)} %fusion.1.refs_0_), channel_id=1, source_target_pairs={{0,2},{1,3},{2,0},{3,1},{4,6},{5,7},{6,4},{7,5},{8,10},{9,11},{10,... | collective-permute-start | bytes 36872 | tf_op jit(solution)/shard_map/ppermute | solution.py:239
  4.4 3.1 %collective-permute-start = (bf16[48,128]{1,0:T(8,128)(2,1)S(1)}, bf16[48,128]{1,0:T(8,128)(2,1)S(1)}, u32[]{:S(2)}, u32[]{:S(2)}) collective-permute-start(bf16[48,128]{1,0:T(8,128)(2,1)S(1)} %fusion.1.refs_0_), channel_id=1, source_target_pairs={{0,1},{1,0},{2,3},{3,2},{4,5},{5,4},{6,7},{7,6},{8,9},{9,8},{10,11... | collective-permute-start | bytes 36872 | tf_op jit(solution)/shard_map/ppermute | solution.py:239
  7.2 0.6 %copy-start.5 = (bf16[48,128]{1,0:T(8,128)(2,1)}, bf16[48,128]{1,0:T(8,128)(2,1)S(1)}, u32[]{:S(2)}) copy-start(bf16[48,128]{1,0:T(8,128)(2,1)S(1)} %collective-permute-done.2.refs_3_) | copy-start | bytes 36868
  7.5 0.6 %copy-start.6 = (bf16[48,128]{1,0:T(8,128)(2,1)}, bf16[48,128]{1,0:T(8,128)(2,1)S(1)}, u32[]{:S(2)}) copy-start(bf16[48,128]{1,0:T(8,128)(2,1)S(1)} %collective-permute-done.1.refs_2_) | copy-start | bytes 36868
  7.5 0.6 %copy-start.7 = (bf16[48,128]{1,0:T(8,128)(2,1)}, bf16[48,128]{1,0:T(8,128)(2,1)S(1)}, u32[]{:S(2)}) copy-start(bf16[48,128]{1,0:T(8,128)(2,1)S(1)} %collective-permute-done.refs_1_) | copy-start | bytes 36868
  17.9 6.3 %collective-permute-start.3 = (f32[32,128]{1,0:T(8,128)}, f32[32,128]{1,0:T(8,128)S(1)}, u32[]{:S(2)}, u32[]{:S(2)}) collective-permute-start(f32[32,128]{1,0:T(8,128)} %get-tuple-element.16), channel_id=1, source_target_pairs={{0,4},{4,0},{8,12},{12,8},{16,20},{20,16},{24,28},{28,24},{1,5},{5... | collective-permute-start | bytes 49160 | tf_op jit(solution)/shard_map/ppermute | solution.py:233
  19.7 6.7 %collective-permute-start.4 = (f32[32,128]{1,0:T(8,128)}, f32[32,128]{1,0:T(8,128)S(1)}, u32[]{:S(2)}, u32[]{:S(2)}) collective-permute-start(f32[32,128]{1,0:T(8,128)} %get-tuple-element.17), channel_id=1, source_target_pairs={{4,8},{8,4},{12,16},{16,12},{20,24},{24,20},{28,0},{0,28},{5,9},{9... | collective-permute-start | bytes 49160 | tf_op jit(solution)/shard_map/ppermute | solution.py:233
  23.3 3.9 %collective-permute-start.5 = (f32[32,128]{1,0:T(8,128)}, f32[32,128]{1,0:T(8,128)S(1)}, u32[]{:S(2)}, u32[]{:S(2)}) collective-permute-start(f32[32,128]{1,0:T(8,128)} %get-tuple-element.18), channel_id=1, source_target_pairs={{0,8},{8,0},{4,12},{12,4},{16,24},{24,16},{20,28},{28,20},{1,9},{9... | collective-permute-start | bytes 49160 | tf_op jit(solution)/shard_map/ppermute | solution.py:233
  23.3 5.7 %collective-permute-start.6 = (f32[32,128]{1,0:T(8,128)}, f32[32,128]{1,0:T(8,128)S(1)}, u32[]{:S(2)}, u32[]{:S(2)}) collective-permute-start(f32[32,128]{1,0:T(8,128)} %get-tuple-element.19), channel_id=1, source_target_pairs={{8,16},{16,8},{12,20},{20,12},{24,0},{0,24},{28,4},{4,28},{9,17},{... | collective-permute-start | bytes 49160 | tf_op jit(solution)/shard_map/ppermute | solution.py:233
  24.2 4.8 %copy-start.1 = (f32[32,128]{1,0:T(8,128)}, f32[32,128]{1,0:T(8,128)S(1)}, u32[]{:S(2)}) copy-start(f32[32,128]{1,0:T(8,128)S(1)} %collective-permute-done.3.refs_3_) | copy-start | bytes 49156
  26.4 2.6 %copy-start.2 = (f32[32,128]{1,0:T(8,128)}, f32[32,128]{1,0:T(8,128)S(1)}, u32[]{:S(2)}) copy-start(f32[32,128]{1,0:T(8,128)S(1)} %collective-permute-done.4.refs_4_) | copy-start | bytes 49156
  27.2 1.8 %copy-start.3 = (f32[32,128]{1,0:T(8,128)}, f32[32,128]{1,0:T(8,128)S(1)}, u32[]{:S(2)}) copy-start(f32[32,128]{1,0:T(8,128)S(1)} %collective-permute-done.5.refs_5_) | copy-start | bytes 49156
  29.0 0.6 %copy-start.4 = (f32[32,128]{1,0:T(8,128)}, f32[32,128]{1,0:T(8,128)S(1)}, u32[]{:S(2)}) copy-start(f32[32,128]{1,0:T(8,128)S(1)} %collective-permute-done.6.refs_6_) | copy-start | bytes 49156
  31.5 3.4 %collective-permute-start.9 = (f32[2048]{0:T(1024)}, f32[2048]{0:T(1024)S(1)}, u32[]{:S(2)}, u32[]{:S(2)}) collective-permute-start(f32[2048]{0:T(1024)} %bitcast.4), channel_id=1, source_target_pairs={{0,3},{1,2},{2,1},{3,0},{4,7},{5,6},{6,5},{7,4},{8,11},{9,10},{10,... | collective-permute-start | bytes 24584 | tf_op jit(solution)/shard_map/ppermute | solution.py:239
  31.5 3.9 %collective-permute-start.8 = (f32[2048]{0:T(1024)}, f32[2048]{0:T(1024)S(1)}, u32[]{:S(2)}, u32[]{:S(2)}) collective-permute-start(f32[2048]{0:T(1024)} %bitcast.5), channel_id=1, source_target_pairs={{0,2},{1,3},{2,0},{3,1},{4,6},{5,7},{6,4},{7,5},{8,10},{9,11},{10,... | collective-permute-start | bytes 24584 | tf_op jit(solution)/shard_map/ppermute | solution.py:239
  33.1 2.4 %collective-permute-start.7 = (f32[2048]{0:T(1024)}, f32[2048]{0:T(1024)S(1)}, u32[]{:S(2)}, u32[]{:S(2)}) collective-permute-start(f32[2048]{0:T(1024)} %bitcast.6), channel_id=1, source_target_pairs={{0,1},{1,0},{2,3},{3,2},{4,5},{5,4},{6,7},{7,6},{8,9},{9,8},{10,11... | collective-permute-start | bytes 24584 | tf_op jit(solution)/shard_map/ppermute | solution.py:239

commit v5 on v3

--- a/solution.py
+++ b/solution.py
@@ -20,6 +20,10 @@
         side = (index // length) % 2
         steps += [length * (1 - 2 * side), length * (2 * side - 1)]
     return steps
+
+
+def near_by(values):
+    return [pltpu.with_memory_space_constraint(value, pltpu.VMEM) for value in values]
 
 
 def ones_where(mask):
@@ -74,10 +78,12 @@
 
 def far_kernel(*refs, share, cells, parents, noff, coefs):
     f32, bf16, i32 = jnp.float32, jnp.bfloat16, jnp.int32
+    row_ref, total_ref = refs[coefs + 4 : coefs + 6]
+    outs = refs[coefs + 6 : coefs + 6 + BLOCKS]
+    scratch = refs[coefs + 6 + BLOCKS :]
     shards = refs[:coefs]
-    ops_ref, tgt_ref, l2l_ref, row_ref, code_ref, total_ref = refs[coefs : coefs + 6]
-    outs = refs[coefs + 6 : coefs + 6 + BLOCKS]
-    poles, spread_parents, poles_t, hot, rhs, acc, terms, picked, far = refs[coefs + 6 + BLOCKS :]
+    ops_ref, tgt_ref, l2l_ref, code_ref = refs[coefs : coefs + 4]
+    poles, spread_parents, poles_t, hot, rhs, acc, terms, picked, far = scratch
     cell_index = lax.axis_index("cells")
     coef_index = lax.axis_index("coef")
     lanes = 4 * share
@@ -85,6 +91,8 @@
     src = lax.broadcasted_iota(i32, (parents, cells), 0)
     dst = lax.broadcasted_iota(i32, (parents, cells), 1)
     spread = ones_where(dst // children == src)
+    acc[...] = jnp.zeros_like(acc)
+    picked[...] = jnp.zeros_like(picked)
     for k in range(coefs):
         at = pl.multiple_of((coef_index ^ k) * share, share)
         shard = shards[k][...]
@@ -93,8 +101,6 @@
             shard[share:, :], spread, (((0,), (0,)), ((), ())), preferred_element_type=f32
         )[:share]
     poles_t[...] = poles[...].astype(f32).T.astype(bf16)
-    acc[...] = jnp.zeros_like(acc)
-    picked[...] = jnp.zeros_like(picked)
     rows = lax.broadcasted_iota(i32, (cells, cells), 0).astype(f32).astype(bf16)
     lane = lax.broadcasted_iota(i32, (cells, lanes), 1)
     is_high = (lane % (2 * share)) < share
@@ -186,9 +192,13 @@
 
 
 def near_kernel(*refs, share, cells):
-    pieces = refs[:BLOCKS]
-    leaf_ref, basis_ref, out_ref, pot_ref = refs[BLOCKS:]
+    leaf_ref, basis_ref = refs[:2]
+    pieces = refs[2 : BLOCKS + 2]
+    out_ref, pot_ref = refs[BLOCKS + 2 :]
     f32, bf16 = jnp.float32, jnp.bfloat16
+    count = leaf_ref.shape[1]
+    rows = lax.broadcasted_iota(jnp.int32, (cells, count), 0)
+    hot = ones_where(rows == leaf_ref[...] - lax.axis_index("cells") * cells)
     leaf = pieces[0][...]
     for piece in pieces[1:]:
         leaf = leaf + piece[...]
@@ -196,9 +206,6 @@
     high = leaf.astype(bf16)
     low = (leaf - high.astype(f32)).astype(bf16)
     both = jnp.concatenate([high, low], axis=0)
-    count = leaf_ref.shape[1]
-    rows = lax.broadcasted_iota(jnp.int32, (cells, count), 0)
-    hot = jnp.where(rows == leaf_ref[...], 1.0, 0.0).astype(bf16)
     columns = jnp.dot(both, hot, preferred_element_type=f32)
     columns = columns[:share] + columns[share:]
     pot_ref[...] = jnp.sum(columns * basis_ref[...].astype(f32), axis=0, keepdims=True)
@@ -207,9 +214,10 @@
 def swapped(value, length, phase):
     count = lax.axis_size("cells")
     pairs = []
-    for low in range(count - length):
+    for low in range(count):
         if (low // length) % 2 == phase:
-            pairs += [(low, low + length), (low + length, low)]
+            high = (low + length) % count
+            pairs += [(low, high), (high, low)]
     return lax.ppermute(value, "cells", pairs)
 
 
@@ -223,7 +231,6 @@
 def on_device(
     multipole, parent_local, m2l_ops, l2l_ops, target_cell, particle_leaf, particle_basis
 ):
-    my_index = lax.axis_index("cells")
     cells = multipole.shape[1]
     parents = parent_local.shape[1]
     coefs = lax.axis_size("coef")
@@ -250,8 +257,8 @@
         functools.partial(
             far_kernel, share=share, cells=cells, parents=parents, noff=noff, coefs=coefs
         ),
-        out_shape=[jax.ShapeDtypeStruct((share, cells), jnp.float32)] * BLOCKS,
-        in_specs=[vmem] * (coefs + 3) + [smem, vmem, smem],
+        out_shape=[pltpu.VMEM((share, cells), jnp.float32)] * BLOCKS,
+        in_specs=[vmem] * (coefs + 4) + [smem, smem],
         out_specs=[vmem] * BLOCKS,
         scratch_shapes=[
             pltpu.VMEM((width, cells), jnp.bfloat16),
@@ -265,23 +272,23 @@
             pltpu.VMEM((2 * REACH * cells, lanes), jnp.float32),
         ],
         name="far",
-    )(*shards, m2l_ops, target_cell, l2l_ops, rows, codes, total)
+    )(*near_by(shards), m2l_ops, target_cell, l2l_ops, codes, rows, total)
     pieces = [blocks[0]]
     for length in range(1, REACH + 1):
         for phase in range(2):
             pieces.append(swapped(blocks[2 * length - 1 + phase], length, phase))
-    index = (particle_leaf - my_index * cells).reshape(1, -1)
+    index = particle_leaf.reshape(1, -1)
     count = index.shape[1]
     leaf_local, partial = pl.pallas_call(
         functools.partial(near_kernel, share=share, cells=cells),
         out_shape=[
             jax.ShapeDtypeStruct((share, cells), jnp.float32),
-            jax.ShapeDtypeStruct((1, count), jnp.float32),
+            pltpu.VMEM((1, count), jnp.float32),
         ],
         in_specs=[vmem] * (BLOCKS + 2),
         out_specs=[vmem] * 2,
         name="near",
-    )(*pieces, index, particle_basis)
+    )(*near_by([index, particle_basis] + pieces))
     sums = from_all(partial.reshape(-1))
     while len(sums) > 1:
         sums = [a + b for a, b in zip(sums[::2], sums[1::2])]

time: 36.7 us -> 31.9 us (0.87)
  the two profiles are of different devices: /device:TPU:13 before, /device:TPU:0 now
where the time goes in v5:
time: 31.9 us; the launch traced here: 31.6 us
  Pallas kernels  11.9 us (37%)
  starting transfers between devices  11.4 us (36%)
  waiting for transfers between devices  6.32 us (20%)
  other arithmetic  1.36 us (4%)
  between operations  0.67 us (2%)
    pallas_call x1, Pallas kernels, on_device(): pl.pallas_call(functools.partial(far_kernel, share=share, cells=cells, pa...  8.52 us
    ppermute x4, starting transfers between devices, swapped(): return lax.ppermute(value, 'cells', pairs)  6.45 us
    ppermute x6, starting transfers between devices, from_all(): lax.ppermute(value, 'coef', [(i, i ^ k) for i in range(count)])  4.95 us
    ppermute x4, waiting for transfers between devices, swapped(): return lax.ppermute(value, 'cells', pairs)  4.26 us
    pallas_call x1, Pallas kernels, on_device(): pl.pallas_call(functools.partial(plan_kernel, cells=cells, noff=noff), ou...  2.75 us
    ppermute x6, waiting for transfers between devices, from_all(): lax.ppermute(value, 'coef', [(i, i ^ k) for i in range(count)])  2.06 us
    concatenate x1, other arithmetic, on_device(): shards = from_all(jnp.concatenate([multipole, flipped], axis=0))  0.75 us
  transfers between devices with their start and end apart: 10, of which 6 were waited for; matrix products, arithmetic and copies ran while one was open for 0% of the time, Pallas kernels for 9%

profile of v5, /device:TPU:0, one launch (start us, length us, event | category | flops | bytes accessed | tf_op | source)
XLA Modules:
  0.0 31.6 jit_solution(8891840497088635211)
XLA Ops:
  0.6 0.0 copy-start
  0.6 0.0 copy-start.1
  0.7 0.8 %fusion.1.refs_0_ = bf16[48,128]{1,0:T(8,128)(2,1)S(1)} fusion(bf16[16,32]{1,0:T(8,128)(2,1)} %bitcast.8, bf16[32,128]{1,0:T(8,128)(2,1)} %param.7), kind=kLoop, calls=%fused_computation.2 | loop fusion | flops 36864 | bytes 21504 | tf_op jit(solution)/shard_map/concatenate | solution.py:239
  1.4 2.4 %collective-permute-start.2 = (bf16[48,128]{1,0:T(8,128)(2,1)S(1)}, bf16[48,128]{1,0:T(8,128)(2,1)S(1)}, u32[]{:S(2)}, u32[]{:S(2)}) collective-permute-start(bf16[48,128]{1,0:T(8,128)(2,1)S(1)} %fusion.1.refs_0_), channel_id=1, source_target_pairs={{0,3},{1,2},{2,1},{3,0},{4,7},{5,6},{6,5},{7,4},{8,11},{9,10},{10,... | collective-permute-start | bytes 36872 | tf_op jit(solution)/shard_map/ppermute | solution.py:227
  3.8 0.6 %collective-permute-start.1 = (bf16[48,128]{1,0:T(8,128)(2,1)S(1)}, bf16[48,128]{1,0:T(8,128)(2,1)S(1)}, u32[]{:S(2)}, u32[]{:S(2)}) collective-permute-start(bf16[48,128]{1,0:T(8,128)(2,1)S(1)} %fusion.1.refs_0_), channel_id=1, source_target_pairs={{0,2},{1,3},{2,0},{3,1},{4,6},{5,7},{6,4},{7,5},{8,10},{9,11},{10,... | collective-permute-start | bytes 36872 | tf_op jit(solution)/shard_map/ppermute | solution.py:227
  4.4 0.1 collective-permute-start
  4.5 2.8 %plan.1 = (s32[1,1024]{1,0:T(1,128)}, s32[1,1024]{1,0:T(1,128)}, s32[8,128]{1,0:T(8,128)}) custom-call(s32[189,128]{1,0:T(8,128)} %refs_5_.1), custom_call_target="tpu_custom_call" | custom-call | tf_op jit(solution)/shard_map/plan/pallas_call | solution.py:243
  7.2 0.0 collective-permute-done.2.refs_3_
  7.2 0.3 collective-permute-done.1.refs_2_
  7.5 0.0 collective-permute-done.refs_1_
  7.5 8.5 %far.1 = (f32[32,128]{1,0:T(8,128)S(1)}, f32[32,128]{1,0:T(8,128)S(1)}, f32[32,128]{1,0:T(8,128)S(1)}, f32[32,128]{1,0:T(8,128)S(1)}, f32[32,128]{1,0:T(8,128)S(1)}) custom-call(bf16[48,128]{1,0:T(8,128)(2,1)S(1)} %fusion.1.refs_0_, bf16[48,128]{1,0:T(8,128)(2,1)S(1)} %collective-permute-done.refs_1_, bf16[48,128]{1,0:T(8,128)(2,1)S(1)} %collective-permute-done.1.refs_2_, ...), custom_call_target="tpu_custom_call" | custom-call | tf_op jit(solution)/shard_map/far/pallas_call | solution.py:256
  16.0 1.7 %collective-permute-start.3 = (f32[32,128]{1,0:T(8,128)S(1)}, f32[32,128]{1,0:T(8,128)S(1)}, u32[]{:S(2)}, u32[]{:S(2)}) collective-permute-start(f32[32,128]{1,0:T(8,128)S(1)} %get-tuple-element.16), channel_id=1, source_target_pairs={{0,4},{4,0},{8,12},{12,8},{16,20},{20,16},{24,28},{28,24},{1,5},{5... | collective-permute-start | bytes 49160 | tf_op jit(solution)/shard_map/ppermute | solution.py:221
  17.7 3.5 %collective-permute-start.4 = (f32[32,128]{1,0:T(8,128)S(1)}, f32[32,128]{1,0:T(8,128)S(1)}, u32[]{:S(2)}, u32[]{:S(2)}) collective-permute-start(f32[32,128]{1,0:T(8,128)S(1)} %get-tuple-element.17), channel_id=1, source_target_pairs={{4,8},{8,4},{12,16},{16,12},{20,24},{24,20},{28,0},{0,28},{5,9},{9... | collective-permute-start | bytes 49160 | tf_op jit(solution)/shard_map/ppermute | solution.py:221
  21.2 0.0 collective-permute-start.5
  21.2 1.3 %collective-permute-start.6 = (f32[32,128]{1,0:T(8,128)S(1)}, f32[32,128]{1,0:T(8,128)S(1)}, u32[]{:S(2)}, u32[]{:S(2)}) collective-permute-start(f32[32,128]{1,0:T(8,128)S(1)} %get-tuple-element.19), channel_id=1, source_target_pairs={{8,16},{16,8},{12,20},{20,12},{24,0},{0,24},{28,4},{4,28},{9,17},{... | collective-permute-start | bytes 49160 | tf_op jit(solution)/shard_map/ppermute | solution.py:221
  22.5 0.0 collective-permute-done.3.refs_3_
  22.5 1.9 %collective-permute-done.4.refs_4_ = f32[32,128]{1,0:T(8,128)S(1)} collective-permute-done((f32[32,128]{1,0:T(8,128)S(1)}, f32[32,128]{1,0:T(8,128)S(1)}, u32[]{:S(2)}, u32[]{:S(2)}) %collective-permute-start.4) | collective-permute-done | bytes 16416 | tf_op jit(solution)/shard_map/ppermute | solution.py:221
  24.4 0.6 %collective-permute-done.5.refs_5_ = f32[32,128]{1,0:T(8,128)S(1)} collective-permute-done((f32[32,128]{1,0:T(8,128)S(1)}, f32[32,128]{1,0:T(8,128)S(1)}, u32[]{:S(2)}, u32[]{:S(2)}) %collective-permute-start.5) | collective-permute-done | bytes 16416 | tf_op jit(solution)/shard_map/ppermute | solution.py:221
  25.0 1.8 %collective-permute-done.6.refs_6_ = f32[32,128]{1,0:T(8,128)S(1)} collective-permute-done((f32[32,128]{1,0:T(8,128)S(1)}, f32[32,128]{1,0:T(8,128)S(1)}, u32[]{:S(2)}, u32[]{:S(2)}) %collective-permute-start.6) | collective-permute-done | bytes 16416 | tf_op jit(solution)/shard_map/ppermute | solution.py:221
  26.8 0.0 copy-done
  26.8 0.0 copy-done.1
  26.8 0.6 %near.1 = (f32[32,128]{1,0:T(8,128)}, f32[1,2048]{1,0:T(1,128)S(1)}) custom-call(s32[1,2048]{1,0:T(1,128)S(1)} %bitcast.3, bf16[32,2048]{1,0:T(8,128)(2,1)S(1)} %copy-done, f32[32,128]{1,0:T(8,128)S(1)} %get-tuple-element.15.refs_2_, f32[32,128]{1,0:T(8,128)S(1)} %collective-permute-done.3.refs_3_, f32[32,128]{1,0:T(8,128)S(1)} %collective-permute-done.4.refs_4_, ...), custom_call_target="tpu_custom_call" | custom-call | tf_op jit(solution)/shard_map/near/pallas_call | solution.py:282
  27.4 0.0 collective-permute-start.9
  27.4 1.5 %collective-permute-start.8 = (f32[2048]{0:T(1024)S(1)}, f32[2048]{0:T(1024)S(1)}, u32[]{:S(2)}, u32[]{:S(2)}) collective-permute-start(f32[2048]{0:T(1024)S(1)} %bitcast.5), channel_id=1, source_target_pairs={{0,2},{1,3},{2,0},{3,1},{4,6},{5,7},{6,4},{7,5},{8,10},{9,11},{10,... | collective-permute-start | bytes 24584 | tf_op jit(solution)/shard_map/ppermute | solution.py:227
  28.9 0.4 %collective-permute-start.7 = (f32[2048]{0:T(1024)S(1)}, f32[2048]{0:T(1024)S(1)}, u32[]{:S(2)}, u32[]{:S(2)}) collective-permute-start(f32[2048]{0:T(1024)S(1)} %bitcast.6), channel_id=1, source_target_pairs={{0,1},{1,0},{2,3},{3,2},{4,5},{5,4},{6,7},{7,6},{8,9},{9,8},{10,11... | collective-permute-start | bytes 24584 | tf_op jit(solution)/shard_map/ppermute | solution.py:227
  29.2 1.2 %collective-permute-done.9 = f32[2048]{0:T(1024)S(1)} collective-permute-done((f32[2048]{0:T(1024)S(1)}, f32[2048]{0:T(1024)S(1)}, u32[]{:S(2)}, u32[]{:S(2)}) %collective-permute-start.9) | collective-permute-done | bytes 8224 | tf_op jit(solution)/shard_map/ppermute | solution.py:227
  30.5 0.5 %collective-permute-done.8 = f32[2048]{0:T(1024)S(1)} collective-permute-done((f32[2048]{0:T(1024)S(1)}, f32[2048]{0:T(1024)S(1)}, u32[]{:S(2)}, u32[]{:S(2)}) %collective-permute-start.8) | collective-permute-done | bytes 8224 | tf_op jit(solution)/shard_map/ppermute | solution.py:227
  31.0 0.0 collective-permute-done.7
  31.0 0.6 %add_add_fusion = f32[2048]{0:T(1024)} fusion(f32[2048]{0:T(1024)S(1)} %collective-permute-done.8, f32[2048]{0:T(1024)S(1)} %collective-permute-done.9, f32[2048]{0:T(1024)S(1)} %bitcast.7, f32[2048]{0:T(1024)S(1)} %collective-permute-done.7), kind=kLoop, calls=%fused_computation.3 | loop fusion | flops 6144 | bytes 40960 | tf_op jit(solution)/shard_map/add | solution.py:294
Async XLA Ops:
  0.6 26.1 %copy-start = (bf16[32,2048]{1,0:T(8,128)(2,1)S(1)}, bf16[32,2048]{1,0:T(8,128)(2,1)}, u32[]{:S(2)}) copy-start(bf16[32,2048]{1,0:T(8,128)(2,1)} %refs_1_.1) | copy-start | bytes 393220
  0.6 26.1 %copy-start.1 = (s32[2048]{0:T(1024)S(1)}, s32[2048]{0:T(1024)}, u32[]{:S(2)}) copy-start(s32[2048]{0:T(1024)} %param.12) | copy-start | bytes 24580
  1.4 5.8 %collective-permute-start.2 = (bf16[48,128]{1,0:T(8,128)(2,1)S(1)}, bf16[48,128]{1,0:T(8,128)(2,1)S(1)}, u32[]{:S(2)}, u32[]{:S(2)}) collective-permute-start(bf16[48,128]{1,0:T(8,128)(2,1)S(1)} %fusion.1.refs_0_), channel_id=1, source_target_pairs={{0,3},{1,2},{2,1},{3,0},{4,7},{5,6},{6,5},{7,4},{8,11},{9,10},{10,... | collective-permute-start | bytes 36872 | tf_op jit(solution)/shard_map/ppermute | solution.py:227
  3.8 3.7 %collective-permute-start.1 = (bf16[48,128]{1,0:T(8,128)(2,1)S(1)}, bf16[48,128]{1,0:T(8,128)(2,1)S(1)}, u32[]{:S(2)}, u32[]{:S(2)}) collective-permute-start(bf16[48,128]{1,0:T(8,128)(2,1)S(1)} %fusion.1.refs_0_), channel_id=1, source_target_pairs={{0,2},{1,3},{2,0},{3,1},{4,6},{5,7},{6,4},{7,5},{8,10},{9,11},{10,... | collective-permute-start | bytes 36872 | tf_op jit(solution)/shard_map/ppermute | solution.py:227
  4.4 3.1 %collective-permute-start = (bf16[48,128]{1,0:T(8,128)(2,1)S(1)}, bf16[48,128]{1,0:T(8,128)(2,1)S(1)}, u32[]{:S(2)}, u32[]{:S(2)}) collective-permute-start(bf16[48,128]{1,0:T(8,128)(2,1)S(1)} %fusion.1.refs_0_), channel_id=1, source_target_pairs={{0,1},{1,0},{2,3},{3,2},{4,5},{5,4},{6,7},{7,6},{8,9},{9,8},{10,11... | collective-permute-start | bytes 36872 | tf_op jit(solution)/shard_map/ppermute | solution.py:227
  16.0 6.5 %collective-permute-start.3 = (f32[32,128]{1,0:T(8,128)S(1)}, f32[32,128]{1,0:T(8,128)S(1)}, u32[]{:S(2)}, u32[]{:S(2)}) collective-permute-start(f32[32,128]{1,0:T(8,128)S(1)} %get-tuple-element.16), channel_id=1, source_target_pairs={{0,4},{4,0},{8,12},{12,8},{16,20},{20,16},{24,28},{28,24},{1,5},{5... | collective-permute-start | bytes 49160 | tf_op jit(solution)/shard_map/ppermute | solution.py:221
  17.7 6.6 %collective-permute-start.4 = (f32[32,128]{1,0:T(8,128)S(1)}, f32[32,128]{1,0:T(8,128)S(1)}, u32[]{:S(2)}, u32[]{:S(2)}) collective-permute-start(f32[32,128]{1,0:T(8,128)S(1)} %get-tuple-element.17), channel_id=1, source_target_pairs={{4,8},{8,4},{12,16},{16,12},{20,24},{24,20},{28,0},{0,28},{5,9},{9... | collective-permute-start | bytes 49160 | tf_op jit(solution)/shard_map/ppermute | solution.py:221
  21.2 3.7 %collective-permute-start.5 = (f32[32,128]{1,0:T(8,128)S(1)}, f32[32,128]{1,0:T(8,128)S(1)}, u32[]{:S(2)}, u32[]{:S(2)}) collective-permute-start(f32[32,128]{1,0:T(8,128)S(1)} %get-tuple-element.18), channel_id=1, source_target_pairs={{0,8},{8,0},{4,12},{12,4},{16,24},{24,16},{20,28},{28,20},{1,9},{9... | collective-permute-start | bytes 49160 | tf_op jit(solution)/shard_map/ppermute | solution.py:221
  21.2 5.5 %collective-permute-start.6 = (f32[32,128]{1,0:T(8,128)S(1)}, f32[32,128]{1,0:T(8,128)S(1)}, u32[]{:S(2)}, u32[]{:S(2)}) collective-permute-start(f32[32,128]{1,0:T(8,128)S(1)} %get-tuple-element.19), channel_id=1, source_target_pairs={{8,16},{16,8},{12,20},{20,12},{24,0},{0,24},{28,4},{4,28},{9,17},{... | collective-permute-start | bytes 49160 | tf_op jit(solution)/shard_map/ppermute | solution.py:221
  27.4 3.1 %collective-permute-start.9 = (f32[2048]{0:T(1024)S(1)}, f32[2048]{0:T(1024)S(1)}, u32[]{:S(2)}, u32[]{:S(2)}) collective-permute-start(f32[2048]{0:T(1024)S(1)} %bitcast.4), channel_id=1, source_target_pairs={{0,3},{1,2},{2,1},{3,0},{4,7},{5,6},{6,5},{7,4},{8,11},{9,10},{10,... | collective-permute-start | bytes 24584 | tf_op jit(solution)/shard_map/ppermute | solution.py:227
  27.4 3.7 %collective-permute-start.8 = (f32[2048]{0:T(1024)S(1)}, f32[2048]{0:T(1024)S(1)}, u32[]{:S(2)}, u32[]{:S(2)}) collective-permute-start(f32[2048]{0:T(1024)S(1)} %bitcast.5), channel_id=1, source_target_pairs={{0,2},{1,3},{2,0},{3,1},{4,6},{5,7},{6,4},{7,5},{8,10},{9,11},{10,... | collective-permute-start | bytes 24584 | tf_op jit(solution)/shard_map/ppermute | solution.py:227
  28.9 2.2 %collective-permute-start.7 = (f32[2048]{0:T(1024)S(1)}, f32[2048]{0:T(1024)S(1)}, u32[]{:S(2)}, u32[]{:S(2)}) collective-permute-start(f32[2048]{0:T(1024)S(1)} %bitcast.6), channel_id=1, source_target_pairs={{0,1},{1,0},{2,3},{3,2},{4,5},{5,4},{6,7},{7,6},{8,9},{9,8},{10,11... | collective-permute-start | bytes 24584 | tf_op jit(solution)/shard_map/ppermute | solution.py:227
